TPU v7x, 256 devices: a whole 4x4x8 slice. The times are simulated.
256 devices in a mesh: blk: 16 (over x_lo, z), tgt: 16 (over y, x_hi, core).
Axes of the slice: x: 4 (x_hi: 2, x_lo: 2; x = x_hi * 2 + x_lo), y: 4, z: 8, core: 2. Of those that a mesh axis runs over, the one named last changes fastest.
Arguments:
- sources: float32 [16384, 128], P('blk'), may hold values from -0.5 to 0.5, as said below
- targets: float32 [65536, 128], P(('blk', 'tgt')), may hold values from -0.5 to 0.5, as said below
- duals_init: float32 [65536], P(('blk', 'tgt')), may hold values from -1.5 to 1.5
Outputs:
- source_duals: float32 [16384], P('blk')
- target_duals: float32 [65536], P(('blk', 'tgt'))
Inputs may be any that keep to these rules, and one draw needn't show every extreme that they name: `sources`: coordinates of the source points. `targets`: coordinates of the target points.
All inputs are finite; a program needn't handle non-finite values.
Results may differ from a plain program's by a relative error of at most 0.0001.
Values sent between devices are 32-bit elements; how exact they have to be, the bound alone decides.
A program may use at most 64 MiB of HBM per device.

v0:
```python
import jax
import jax.numpy as jnp
from jax import lax
from jax.sharding import Mesh
from jax.sharding import PartitionSpec as P

ITERS = 2
BLK = ("blk_0", "blk_1")
BLK_TGT = ("blk_0", "blk_1", "tgt")


EPS = 0.05


def in_order(blocks, dim):
    shape = list(blocks.shape[1:])
    shape[dim] *= blocks.shape[0]
    return jnp.moveaxis(blocks, 0, dim).reshape(shape)


def all_blocks(x, axes, turns):
    blocks = x
    for k in turns:
        blocks = lax.all_gather(blocks, axes[k])
    done = turns[::-1]
    back = [done.index(k) for k in range(len(axes))]
    blocks = blocks.transpose(*back, *range(len(axes), blocks.ndim))
    return blocks.reshape(-1, *x.shape)


def gather_axes(x, axes, turns, dim):
    return in_order(all_blocks(x, axes, turns), dim)


def sent_to_all(x, axis):
    count = lax.axis_size(axis)
    return lax.all_to_all(jnp.broadcast_to(x[None], (count, *x.shape)), axis, 0, 0, tiled=True)


def collect(x, axis, dim):
    return in_order(sent_to_all(x, axis), dim)


def gathered_once(x, axis):
    leaves = jax.tree.leaves(x)
    turns = sorted(range(len(leaves)), key=lambda k: -leaves[k].size)
    width = (1, *leaves[turns[0]].shape)[-1]
    lines = [
        jnp.pad(leaves[k].reshape(-1), (0, -leaves[k].size % width)).reshape(-1, width)
        for k in turns
    ]
    both, at, found = (sent_to_all(jnp.concatenate(lines), axis), 0, {})
    for k, line in zip(turns, lines):
        section = both[:, at : at + len(line)].reshape(len(both), -1)
        found[k] = section[:, : leaves[k].size].reshape(-1, *leaves[k].shape)
        at += len(line)
    numbers = iter(range(len(leaves)))
    return jax.tree.map(lambda _: found[next(numbers)], x)


def gathered_by_type(x, axis):
    leaves, found = (jax.tree.leaves(x), {})
    for first, a in enumerate(leaves):
        if first not in found:
            alike = [k for k, b in enumerate(leaves) if b.dtype == a.dtype]
            got = (
                gathered_once([leaves[k] for k in alike], axis)
                if len(alike) > 1
                else [sent_to_all(a, axis)]
            )
            for k, b in zip(alike, got):
                found[k] = b
    numbers = iter(range(len(leaves)))
    return jax.tree.map(lambda _: found[next(numbers)], x)


def folded_in_pairs(pieces, combine):
    while len(jax.tree.leaves(pieces)[0]) > 1:
        pieces = jax.vmap(combine)(
            *(jax.tree.map(lambda part: part[side::2], pieces) for side in (0, 1))
        )
    return jax.tree.map(lambda part: part[0], pieces)


def joined_all(x, axis, combine):
    pieces = gathered_by_type(x, axis)
    return folded_in_pairs(pieces, combine)


def over_copies(x, axis):
    everything = sent_to_all(x, axis)
    return jnp.max(everything, axis=0)


def split_up(x, dim, count):
    shape = x.shape
    blocks = x.reshape(*shape[:dim], count, shape[dim] // count, *shape[dim + 1 :])
    return jnp.moveaxis(blocks, dim, 0)


def sent_and_summed(x, axis, dim):
    count = lax.axis_size(axis)
    blocks = lax.all_to_all(split_up(x, dim, count), axis, 0, 0, tiled=True)
    return jnp.sum(blocks, axis=0)


def cost_of(left, left_norm, right, right_norm):
    cross = jnp.dot(
        left, right.T, preferred_element_type=jnp.float32, precision=lax.Precision.HIGHEST
    )
    return left_norm[:, None] + right_norm[None, :] - 2.0 * cross


def combine(first, second):
    highest = jnp.maximum(first[0], second[0])
    return (
        highest,
        first[1] * jnp.exp(first[0] - highest) + second[1] * jnp.exp(second[0] - highest),
    )


def body(sources, targets, duals_init):
    src_norm = jnp.sum(sources * sources, axis=1)
    rows_here = sources.shape[0]
    cols_here = targets.shape[0]
    total_dst = cols_here * lax.axis_size(BLK) * lax.axis_size("tgt")
    total_src = rows_here * lax.axis_size(BLK)
    target_pots = duals_init
    source_pots = jnp.zeros_like(src_norm)
    group_rows = gather_axes(targets, BLK, (0, 1), 0)
    group_norm = jnp.sum(group_rows * group_rows, axis=1)
    cost_tile = cost_of(sources, src_norm, group_rows, group_norm)
    for repeat in range(ITERS):
        group_pots = collect(target_pots, BLK, 0)
        scores = (group_pots[None, :] - cost_tile) / EPS
        maxima = jnp.max(scores, axis=1)
        totals = jnp.sum(jnp.exp(scores - maxima[:, None]), axis=1)
        maxima, totals = joined_all((maxima, totals), "tgt", combine)
        source_pots = EPS * -jnp.log(jnp.float32(total_dst)) - EPS * (maxima + jnp.log(totals))
        col_scores = (source_pots[:, None] - cost_tile) / EPS
        col_high = over_copies(jnp.max(col_scores, axis=0), BLK)
        col_part = jnp.sum(jnp.exp(col_scores - col_high[None, :]), axis=0)
        col_total = sent_and_summed(col_part, BLK, 0)
        own_high = lax.dynamic_slice_in_dim(col_high, lax.axis_index(BLK) * cols_here, cols_here, 0)
        target_pots = EPS * -jnp.log(jnp.float32(total_src)) - EPS * (own_high + jnp.log(col_total))
    return (source_pots, target_pots)


def solution(mesh):
    finer = Mesh(mesh.devices.reshape(2, 8, mesh.shape["tgt"]), ("blk_0", "blk_1", "tgt"))
    return jax.shard_map(
        body,
        mesh=finer,
        in_specs=(P(BLK, None), P(BLK_TGT, None), P(BLK_TGT)),
        out_specs=(P(BLK), P(BLK_TGT)),
        check_vma=False,
    )
```

profile of v0, /device:TPU:1, one launch (start us, length us, event | category | flops | bytes accessed | tf_op | source)
XLA Modules:
  0.0 236.0 jit_solution(17945655105315867702)
XLA Ops:
  7.2 6.9 %all-gather = f32[512,128]{1,0:T(8,128)} all-gather(f32[256,128]{1,0:T(8,128)} %param.4), channel_id=2, replica_groups=mesh['blk_0'=2,'blk_1'=8,'tgt'=16] {'blk_0'}, dimensions={0}, use_global_device_ids=true | all-gather | bytes 393216 | tf_op jit(solution)/shard_map/all_gather | solution.py:24
  14.1 1.3 broadcast_in_dim.12
  15.4 9.1 %all-to-all-start = ((f32[16,1,256]{2,1,0:T(1,128)}), f32[16,1,256]{2,1,0:T(1,128)S(1)}, u32[]{:S(2)}, u32[]{:S(2)}) async-start(f32[16,1,256]{2,1,0:T(1,128)} %broadcast_in_dim.12), calls=%async_computation | async-start | bytes 32768 | tf_op jit(solution)/shard_map/all_to_all | solution.py:37
  24.6 1.2 multiply_reduce_fusion.1
  25.8 29.2 %all-gather.4.cloned.1.call-done = f32[16,256,128]{2,1,0:T(8,128)} async-done(((f32[2,256,128]{2,1,0:T(8,128)}), f32[16,256,128]{2,1,0:T(8,128)}) %all-gather.4.cloned.1.call-update) | async-done | bytes 2097168 | tf_op jit(solution)/shard_map/all_gather | solution.py:24
  55.1 2.2 multiply_reduce_fusion
  57.3 1.7 copy.21
  59.1 17.7 %fusion = (f32[1024]{0:T(1024)S(1)}, f32[1024,4096]{1,0:T(8,128)S(1)}) fusion(f32[4096]{0:T(1024)S(1)} %bitcast.41, f32[1024,128]{1,0:T(8,128)} %param.3, f32[4096,128]{1,0:T(8,128)S(1)} %bitcast.33, f32[4096]{0:T(1024)S(1)} %bitcast.54, f32[1024]{0:T(1024)S(1)} %multiply_reduce_fusion.1), kind=kOutput, calls=%fused_computation.9 | convolution fusion | flops 6467615744 | bytes 19439616 | tf_op jit(solution)/shard_map/dot_general | solution.py:108
  76.7 5.7 %copy-done = f32[1024,4096]{1,0:T(8,128)} copy-done((f32[1024,4096]{1,0:T(8,128)}, f32[1024,4096]{1,0:T(8,128)S(1)}, u32[]{:S(2)}) %copy-start) | copy-done | bytes 16777240
  82.5 4.1 %exponential_reduce_fusion.3 = f32[1024]{0:T(1024)S(1)} fusion(f32[1024,4096]{1,0:T(8,128)S(1)} %get-tuple-element.19, f32[1024]{0:T(1024)S(1)} %get-tuple-element.18, f32[4096]{0:T(1024)S(1)} %bitcast.42), kind=kLoop, calls=%fused_computation.6 | loop fusion | flops 16776192 | bytes 16801792 | tf_op jit(solution)/shard_map/reduce_sum | solution.py:137
  86.6 19.0 %all_to_all.52 = f32[16,2,1024]{2,1,0:T(2,128)S(1)} all-to-all(f32[16,2,1024]{2,1,0:T(2,128)S(1)} %broadcast_in_dim.13), channel_id=1, replica_groups=mesh['blk_0'=2,'blk_1'=8,'tgt'=16] {'tgt'}, dimensions={0} | all-to-all | bytes 262144 | tf_op jit(solution)/shard_map/all_to_all | solution.py:37
  106.1 7.7 %fusion.1 = f32[4096]{0:T(1024)S(1)} fusion(f32[1024,4096]{1,0:T(8,128)} %copy-done, f32[1024]{0:T(1024)S(1)} %bitcast.48), kind=kLoop, calls=%fused_computation.10 | loop fusion | flops 12578816 | bytes 16797696 | tf_op jit(solution)/shard_map/reduce_max | solution.py:141
  114.1 12.7 %all_to_all.53 = f32[16,1,4096]{2,1,0:T(1,128)S(1)} all-to-all(f32[16,1,4096]{2,1,0:T(1,128)S(1)} %broadcast_in_dim.14), channel_id=1, replica_groups=mesh['blk_0'=2,'blk_1'=8,'tgt'=16] {'blk_0','blk_1'}, dimensions={0} | all-to-all | bytes 524288 | tf_op jit(solution)/shard_map/all_to_all | solution.py:37
  126.9 8.3 %exponential_reduce_fusion.2 = f32[4096]{0:T(1024)} fusion(f32[1024,4096]{1,0:T(8,128)} %copy-done, f32[4096]{0:T(1024)S(1)} %reduce_max.56, f32[1024]{0:T(1024)S(1)} %bitcast.49), kind=kLoop, calls=%fused_computation.4 | loop fusion | flops 16773120 | bytes 16814080 | tf_op jit(solution)/shard_map/reduce_sum | solution.py:142
  135.3 5.4 %all-to-all-start.3 = ((f32[16,1,256]{2,1,0:T(1,128)}), f32[16,1,256]{2,1,0:T(1,128)S(1)}, u32[]{:S(2)}, u32[]{:S(2)}) async-start(f32[16,1,256]{2,1,0:T(1,128)} %bitcast.10), calls=%async_computation.3 | async-start | bytes 32768 | tf_op jit(solution)/shard_map/all_to_all | solution.py:103
  140.7 7.3 %all-to-all-done.3 = f32[16,1,256]{2,1,0:T(1,128)S(1)} async-done(((f32[16,1,256]{2,1,0:T(1,128)}), f32[16,1,256]{2,1,0:T(1,128)S(1)}, u32[]{:S(2)}, u32[]{:S(2)}) %all-to-all-start.3) | async-done | bytes 16416 | tf_op jit(solution)/shard_map/all_to_all | solution.py:103
  148.2 9.9 %all_to_all.54 = f32[16,1,256]{2,1,0:T(1,128)S(1)} all-to-all(f32[16,1,256]{2,1,0:T(1,128)S(1)} %broadcast_in_dim.15), channel_id=1, replica_groups=mesh['blk_0'=2,'blk_1'=8,'tgt'=16] {'blk_0','blk_1'}, dimensions={0} | all-to-all | bytes 32768 | tf_op jit(solution)/shard_map/all_to_all | solution.py:37
  158.1 7.6 %fusion.2 = f32[1024]{0:T(1024)S(1)} fusion(f32[1024,4096]{1,0:T(8,128)} %copy-done, f32[4096]{0:T(1024)S(1)} %bitcast.39), kind=kLoop, calls=%fused_computation.11 | loop fusion | flops 12581888 | bytes 16797696 | tf_op jit(solution)/shard_map/reduce_max | solution.py:136
  165.6 7.9 %exponential_reduce_fusion.1 = f32[1024]{0:T(1024)S(1)} fusion(f32[1024,4096]{1,0:T(8,128)} %copy-done, f32[1024]{0:T(1024)S(1)} %fusion.2, f32[4096]{0:T(1024)S(1)} %bitcast.40), kind=kLoop, calls=%fused_computation.2 | loop fusion | flops 16776192 | bytes 16801792 | tf_op jit(solution)/shard_map/reduce_sum | solution.py:137
  173.6 14.4 %all_to_all.55 = f32[16,2,1024]{2,1,0:T(2,128)S(1)} all-to-all(f32[16,2,1024]{2,1,0:T(2,128)S(1)} %broadcast_in_dim.16), channel_id=1, replica_groups=mesh['blk_0'=2,'blk_1'=8,'tgt'=16] {'tgt'}, dimensions={0} | all-to-all | bytes 262144 | tf_op jit(solution)/shard_map/all_to_all | solution.py:37
  188.5 7.7 %fusion.3 = f32[4096]{0:T(1024)S(1)} fusion(f32[1024,4096]{1,0:T(8,128)} %copy-done, f32[1024]{0:T(1024)S(1)} %bitcast.45), kind=kLoop, calls=%fused_computation.12 | loop fusion | flops 12578816 | bytes 16797696 | tf_op jit(solution)/shard_map/reduce_max | solution.py:141
  196.4 11.6 %all_to_all.56 = f32[16,1,4096]{2,1,0:T(1,128)S(1)} all-to-all(f32[16,1,4096]{2,1,0:T(1,128)S(1)} %broadcast_in_dim.17), channel_id=1, replica_groups=mesh['blk_0'=2,'blk_1'=8,'tgt'=16] {'blk_0','blk_1'}, dimensions={0} | all-to-all | bytes 524288 | tf_op jit(solution)/shard_map/all_to_all | solution.py:37
  208.2 7.7 %exponential_reduce_fusion = f32[4096]{0:T(1024)S(1)} fusion(f32[1024,4096]{1,0:T(8,128)} %copy-done, f32[4096]{0:T(1024)S(1)} %reduce_max.59, f32[1024]{0:T(1024)S(1)} %bitcast.46), kind=kLoop, calls=%fused_computation | loop fusion | flops 16773120 | bytes 16814080 | tf_op jit(solution)/shard_map/reduce_sum | solution.py:142
  216.0 12.5 %all_to_all.57 = f32[16,1,256]{2,1,0:T(1,128)S(1)} all-to-all(f32[16,1,256]{2,1,0:T(1,128)S(1)} %bitcast.43), channel_id=1, replica_groups=mesh['blk_0'=2,'blk_1'=8,'tgt'=16] {'blk_0','blk_1'}, dimensions={0} | all-to-all | bytes 32768 | tf_op jit(solution)/shard_map/all_to_all | solution.py:103
  (58 shorter events, 2.7 us)
Async XLA Ops:
  7.2 47.9 %all-gather.4.cloned.1.call-start = ((), (), s32[]{:S(2)}) async-start(), calls=%async_computation.8 | async-start | bytes 2359296 | tf_op jit(solution)/shard_map/all_gather | solution.py:24
  15.4 43.6 %all-to-all-start = ((f32[16,1,256]{2,1,0:T(1,128)}), f32[16,1,256]{2,1,0:T(1,128)S(1)}, u32[]{:S(2)}, u32[]{:S(2)}) async-start(f32[16,1,256]{2,1,0:T(1,128)} %broadcast_in_dim.12), calls=%async_computation | async-start | bytes 32768 | tf_op jit(solution)/shard_map/all_to_all | solution.py:37
  76.7 5.7 %copy-start = (f32[1024,4096]{1,0:T(8,128)}, f32[1024,4096]{1,0:T(8,128)S(1)}, u32[]{:S(2)}) copy-start(f32[1024,4096]{1,0:T(8,128)S(1)} %get-tuple-element.19) | copy-start | bytes 50331652
  135.3 12.8 %all-to-all-start.3 = ((f32[16,1,256]{2,1,0:T(1,128)}), f32[16,1,256]{2,1,0:T(1,128)S(1)}, u32[]{:S(2)}, u32[]{:S(2)}) async-start(f32[16,1,256]{2,1,0:T(1,128)} %bitcast.10), calls=%async_computation.3 | async-start | bytes 32768 | tf_op jit(solution)/shard_map/all_to_all | solution.py:103
  188.5 27.5 %copy-start.1 = (f32[1,1024]{1,0:T(1,128)}, f32[1,1024]{1,0:T(1,128)S(1)}, u32[]{:S(2)}) copy-start(f32[1,1024]{1,0:T(1,128)S(1)} %multiply_subtract_fusion.1) | copy-start | bytes 12292
Sparse Core Ops, SparseCore 0:
  14.3 40.7 all-gather.3
where the time goes:
time: 237 us; the launch traced here: 236 us
  blocking collectives  86.9 us (37%)
  other arithmetic  55.9 us (24%)
  waiting for transfers between devices  36.6 us (15%)
  matrix products  17.7 us (7%)
  starting transfers between devices  14.6 us (6%)
  between operations  14.3 us (6%)
  local copies, waits for them, and re-layouts  10 us (4%)
    all_to_all x5, blocking collectives, sent_to_all(): lax.all_to_all(jnp.broadcast_to(x[None], (count, *x.shape)), axis, 0, 0,...  67.5 us
    all_gather x1, waiting for transfers between devices, all_blocks(): blocks = lax.all_gather(blocks, axes[k])  29.2 us
    dot_general x1, matrix products, cost_of(): jnp.dot(left, right.T, preferred_element_type=jnp.float32, precision=lax....  17.7 us
    reduce_sum x2, other arithmetic, body(): col_part = jnp.sum(jnp.exp(col_scores - col_high[None, :]), axis=0)  16.1 us
    reduce_max x2, other arithmetic, body(): col_high = over_copies(jnp.max(col_scores, axis=0), BLK)  15.4 us
    all_to_all x1, blocking collectives, sent_and_summed(): blocks = lax.all_to_all(split_up(x, dim, count), axis, 0, 0, tiled=True)  12.5 us
    reduce_sum x2, other arithmetic, body(): totals = jnp.sum(jnp.exp(scores - maxima[:, None]), axis=1)  12 us
    all_to_all x1, starting transfers between devices, sent_to_all(): lax.all_to_all(jnp.broadcast_to(x[None], (count, *x.shape)), axis, 0, 0,...  9.13 us
  transfers between devices with their start and end apart: 3, of which 2 were waited for; matrix products, arithmetic and copies ran while one was open for 3% of the time, Pallas kernels for 0%

commit v1 on v0

v1 whole, which is shorter than its diff:
```python
import functools
import math

import jax
import jax.numpy as jnp
from jax import lax
from jax.experimental import pallas as pl
from jax.experimental.pallas import tpu as pltpu
from jax.sharding import PartitionSpec as P

EPS = 0.05
LOG2E = math.log2(math.e)
SCALE = LOG2E / EPS
MESH = pl.DeviceIdType.MESH
NZ = 8
NP = 16
ROWS = 1024
COLS = 256
BLOCKS = 16
HEAD = 8
D = 128
LANES = 128
CHUNK = 128
CUTS = ((0, HEAD + CHUNK), (HEAD + CHUNK, CHUNK))
F32 = jnp.float32


def lse2(parts):
    high = functools.reduce(jnp.maximum, parts)
    total = functools.reduce(jnp.add, [jnp.exp2(p - high) for p in parts])
    return high + jnp.log2(total)


def kernel(
    log_src, log_dst,
    src_ref, tgt_ref, g0_ref, f_ref, g_ref,
    tile, blocks, rows_in, lhs, acc, wide,
    row_stat, col_stat, beta, delta, weight,
    row_buf, pair_buf, z_buf, own_buf, fin_buf, f_own, f_pair,
    ring_send, ring_recv, d2d_send, d2d_recv, x_send, x_recv,
    row_send, row_recv, z_send, z_recv, pair_send, pair_recv,
):
    blk, tgt = lax.axis_index("blk"), lax.axis_index("tgt")
    x_lo, z = blk // NZ, lax.rem(blk, NZ)
    core, x_hi, y = lax.rem(tgt, 2), lax.rem(tgt // 2, 2), tgt // 4
    pair = (blk, tgt + 1 - 2 * core)
    me = x_lo * 8 + tgt // 2

    def on_plane(q):
        return (q // 8) * NZ + z, lax.rem(q, 8) * 2 + core

    def on_ring(other):
        return x_lo * NZ + other, tgt

    def beside(step):
        x = lax.rem(2 * x_hi + x_lo + step + 4, 4)
        return lax.rem(x, 2) * NZ + z, y * 4 + (x // 2) * 2 + x_lo

    swaps = core != x_lo
    left, right = beside(-1), beside(1)

    barrier = pltpu.get_barrier_semaphore()
    for k in range(1, NP):
        pl.semaphore_signal(barrier, inc=1, device_id=on_plane(lax.rem(me + k, NP)), device_id_type=MESH)
    for k in range(1, NZ):
        pl.semaphore_signal(barrier, inc=1, device_id=on_ring(lax.rem(z + k, NZ)), device_id_type=MESH)
    pl.semaphore_signal(barrier, inc=1, device_id=pair, device_id_type=MESH)

    @pl.when(swaps)
    def _():
        for there in (left, right):
            pl.semaphore_signal(barrier, inc=1, device_id=there, device_id_type=MESH)

    own = core * NZ + z
    mine = tgt_ref[...]
    for half in range(2):
        part = mine[half * LANES : (half + 1) * LANES, :]
        norm = jnp.sum((part * part).T, axis=0, keepdims=True)
        blocks[own, half : half + 1, :] = SCALE * (g0_ref[half : half + 1, :] - norm)
    blocks[own, HEAD:, :] = mine

    pl.semaphore_wait(barrier, NP - 1 + NZ - 1 + 1 + 2 * swaps.astype(jnp.int32))

    def copy(src, dst, send, recv, where):
        return pltpu.make_async_remote_copy(
            src_ref=src, dst_ref=dst, send_sem=send, recv_sem=recv, device_id=where, device_id_type=MESH
        )

    def piece(b, k):
        start, size = CUTS[k]
        return blocks.at[b, pl.ds(start, size), :]

    def ring_copy(way, step, k, b):
        to = on_ring(lax.rem(z + (1 if way == 0 else NZ - 1), NZ))
        slot = 2 * (step - 1) + (k if step < 4 else 0)
        return copy(piece(b, k), piece(b, k), ring_send.at[way, slot], ring_recv.at[way, slot], to)

    def pair_copy(b, k):
        at = lax.rem(b, NZ) * 2 + k
        return copy(piece(b, k), piece(b, k), d2d_send.at[at], d2d_recv.at[at], pair)

    def swap_copy(side):
        at = pl.ds(side * (ROWS // 2), ROWS // 2)
        return copy(src_ref.at[at, :], rows_in.at[at, :], x_send.at[side], x_recv.at[side], (left, right)[side])

    for k in range(2):
        for way in range(2):
            ring_copy(way, 1, k, own).start()

    @pl.when(swaps)
    def _():
        for side in range(2):
            swap_copy(side).start()

    for k in range(2):
        pair_copy(own, k).start()

    @pl.when(jnp.logical_not(swaps))
    def _():
        rows_in[...] = src_ref[...]

    def origin(way, step):
        return lax.rem(z + (NZ - step if way == 0 else step), NZ)

    def receive(step, k):
        for way in range(2):
            if step == 4 and k != way:
                continue
            b = core * NZ + origin(way, step)
            ring_copy(way, step, k, b).wait_recv()
            if step < 3 or (step == 3 and k == way):
                ring_copy(way, step + 1, k, b).start()
            pair_copy(b, k).start()

    def prepare():
        @pl.when(swaps)
        def _():
            for side in range(2):
                swap_copy(side).wait()

        for r in range(ROWS // LANES):
            rows = rows_in[r * LANES : (r + 1) * LANES, :] * (2 * SCALE)
            high = rows.astype(jnp.bfloat16)
            low = (rows - high.astype(F32)).astype(jnp.bfloat16)
            lhs[r * LANES : (r + 1) * LANES, :] = jnp.concatenate([high, low, high, low], axis=1)
        acc[...] = jnp.full_like(acc, -jnp.inf)

    def scores(b):
        t = blocks[b, HEAD:, :]
        high = t.astype(jnp.bfloat16)
        low = (t - high.astype(F32)).astype(jnp.bfloat16)
        rhs = jnp.concatenate([high, high, low, low], axis=1)
        head = jnp.concatenate([blocks[b, 0:1, :], blocks[b, 1:2, :]], axis=1)
        out = lax.dot_general(lhs[...], rhs, (((1,), (1,)), ((), ())), preferred_element_type=F32) + head
        tile[b] = out
        acc[...] = jnp.maximum(acc[...], jnp.maximum(out[:, :LANES], out[:, LANES:]))

    def scores_from_pair(zb, waits=True):
        if waits:
            for k in range(2):
                pair_copy((1 - core) * NZ + zb, k).wait_recv()
        scores((1 - core) * NZ + zb)

    def own_and_pair(step):
        def one(i, carry):
            zb = lax.rem(z + jnp.where(i == 0, NZ - step, step), NZ)
            scores(core * NZ + zb)
            scores_from_pair(zb)
            return carry

        lax.fori_loop(0, 2, one, 0)

    receive(1, 0)
    receive(1, 1)
    prepare()
    scores(own)
    scores_from_pair(z)
    receive(2, 0)
    receive(2, 1)
    own_and_pair(1)
    receive(3, 0)
    receive(3, 1)
    own_and_pair(2)
    receive(4, 0)
    receive(4, 1)
    own_and_pair(3)
    far = lax.rem(z + 4, NZ)
    scores(core * NZ + far)
    scores_from_pair(far)

    def narrow(reduce, r):
        return reduce(acc[r * LANES : (r + 1) * LANES, :].T, axis=0, keepdims=True)

    def spread(row):
        for r in range(ROWS // LANES):
            wide[r * LANES : (r + 1) * LANES, :] = jnp.broadcast_to(row[r : r + 1, :], (LANES, LANES)).T

    def row_copy(phase, k):
        there = on_plane(lax.rem(me + k, NP))
        slot = row_buf.at[phase, me]
        return copy(slot, slot, row_send.at[phase, k], row_recv.at[phase, me], there)

    def across_plane(phase, reduce):
        for r in range(ROWS // LANES):
            row_buf[phase, me, r : r + 1, :] = narrow(reduce, r)

        def send(k, carry):
            row_copy(phase, k).start()
            return carry

        lax.fori_loop(1, NP, send, 0)

        def arrive(k, carry):
            q = lax.rem(me + k, NP)
            slot = row_buf.at[phase, q]
            copy(slot, slot, row_send.at[phase, k], row_recv.at[phase, q], on_plane(q)).wait_recv()
            return carry

        lax.fori_loop(1, NP, arrive, 0)
        return reduce(row_buf[phase], axis=0)

    high = across_plane(0, jnp.max)
    spread(high)

    steps = ROWS // CHUNK

    def by_groups(x):
        return x.reshape(CHUNK // 8, 8, LANES)

    def column_pass(into, term, reduce, start):
        def block(b, carry):
            def some(r, total):
                at = pl.ds(pl.multiple_of(r * CHUNK, CHUNK), CHUNK)
                w = wide[at, :]
                return tuple(
                    reduce[0](total[h], reduce[1](by_groups(term(tile[b, at, h * LANES : (h + 1) * LANES], w)), axis=0))
                    for h in range(2)
                )

            total = lax.fori_loop(0, steps, some, (jnp.full((8, LANES), start, F32),) * 2)
            for h in range(2):
                into[pl.ds(2 * b + h, 1), :] = reduce[1](total[h], axis=0, keepdims=True)
            return carry

        lax.fori_loop(0, BLOCKS, block, 0)

    column_pass(beta, lambda t, w: t - w, (jnp.maximum, jnp.max), -jnp.inf)
    weight[...] = jnp.exp2(beta[...])

    def row_pass(first):
        def rows(r, carry):
            at = pl.ds(pl.multiple_of(r * CHUNK, CHUNK), CHUNK)

            def block(b, total):
                for h in range(2):
                    cut = slice(h * LANES, (h + 1) * LANES)
                    entry = tile[b, at, cut]
                    if first:
                        entry = jnp.exp2(entry - wide[at, :] - beta[pl.ds(2 * b + h, 1), :])
                        tile[b, at, cut] = entry
                    total = total + entry * weight[pl.ds(2 * b + h, 1), :]
                return total

            acc[at, :] = lax.fori_loop(0, BLOCKS, block, jnp.zeros((CHUNK, LANES), F32))
            return carry

        lax.fori_loop(0, steps, rows, 0)

    def halves(step):
        return pl.ds(pl.multiple_of(step * BLOCKS, BLOCKS), BLOCKS)

    def with_pair(phase):
        column_pass(col_stat, lambda t, w: t * w, (jnp.add, jnp.sum), 0.0)
        col_stat[...] = beta[...] + jnp.log2(col_stat[...])
        swap = copy(
            col_stat.at[halves(1 - core), :], pair_buf.at[phase], pair_send.at[phase], pair_recv.at[phase], pair
        )
        swap.start()
        swap.wait()
        return lse2([col_stat[halves(core), :], pair_buf[phase]])

    def round_ring(phase, src, dst):
        def send(k, carry):
            other = lax.rem(z + k, NZ)
            copy(src(other), dst(z), z_send.at[phase, k], z_recv.at[phase, z], on_ring(other)).start()
            return carry

        lax.fori_loop(1, NZ, send, 0)

        def arrive(k, carry):
            other = lax.rem(z + k, NZ)
            copy(src(other), dst(other), z_send.at[phase, k], z_recv.at[phase, other], on_ring(other)).wait_recv()
            return carry

        lax.fori_loop(1, NZ, arrive, 0)

    row_pass(True)
    sums = across_plane(1, jnp.sum)
    spread(jnp.exp2(-log_dst - jnp.log2(sums)))
    z_buf[z] = with_pair(0)
    round_ring(0, lambda other: z_buf.at[z], lambda other: z_buf.at[other])
    delta[halves(core), :] = -log_src - lse2([z_buf[k] for k in range(NZ)])
    half = delta.at[halves(core), :]
    give = copy(half, half, pair_send.at[2], pair_recv.at[2], pair)
    give.start()
    give.wait()
    weight[...] = jnp.exp2(delta[...] + beta[...])

    row_pass(False)
    sums = across_plane(2, jnp.sum)
    spread(jnp.exp2(-log_dst - jnp.log2(sums)))
    for r in range(ROWS // LANES):
        rows = rows_in[r * LANES : (r + 1) * LANES, :]
        row_stat[r : r + 1, :] = jnp.sum((rows * rows).T, axis=0, keepdims=True)
    f_own[...] = row_stat[...] - (log_dst + jnp.log2(sums) + high) / SCALE

    hand = copy(f_own, f_pair, pair_send.at[3], pair_recv.at[3], pair)
    hand.start()
    joined = with_pair(1)
    for k in range(NZ):
        own_buf[k] = joined[2 * k : 2 * k + 2, :]
    fin_buf[z] = own_buf[z]
    round_ring(1, lambda other: own_buf.at[other], lambda other: fin_buf.at[other])
    g_ref[...] = g0_ref[...] - (log_src + lse2([fin_buf[k] for k in range(NZ)])) / SCALE
    hand.wait()
    f_ref[...] = jnp.where(swaps, f_pair[...], f_own[...])

    for step in range(1, 5):
        for k in range(2):
            for way in range(2):
                if step < 4 or k == way:
                    ring_copy(way, step, k, own).wait_send()
    for b in range(NZ):
        for k in range(2):
            pair_copy(core * NZ + b, k).wait_send()
    for phase in range(3):
        def left_row(k, carry):
            row_copy(phase, k).wait_send()
            return carry

        lax.fori_loop(1, NP, left_row, 0)
    for phase in range(2):
        def left_ring(k, carry):
            src = z_buf.at[z] if phase == 0 else own_buf.at[z]
            copy(src, src, z_send.at[phase, k], z_recv.at[phase, z], on_ring(z)).wait_send()
            return carry

        lax.fori_loop(1, NZ, left_ring, 0)


def body(sources, targets, duals_init):
    n_src = sources.shape[0] * lax.axis_size("blk")
    n_dst = targets.shape[0] * lax.axis_size("blk") * lax.axis_size("tgt")
    vmem = pl.BlockSpec(memory_space=pltpu.VMEM)
    dma = pltpu.SemaphoreType.DMA
    f, g = pl.pallas_call(
        functools.partial(kernel, math.log2(n_src), math.log2(n_dst)),
        out_shape=(jax.ShapeDtypeStruct((8, LANES), F32), jax.ShapeDtypeStruct((2, LANES), F32)),
        in_specs=[vmem] * 3,
        out_specs=(vmem, vmem),
        scratch_shapes=[
            pltpu.VMEM((BLOCKS, ROWS, COLS), F32),
            pltpu.VMEM((BLOCKS, HEAD + COLS, D), F32),
            pltpu.VMEM((ROWS, D), F32),
            pltpu.VMEM((ROWS, 4 * D), jnp.bfloat16),
            pltpu.VMEM((ROWS, LANES), F32),
            pltpu.VMEM((ROWS, LANES), F32),
            pltpu.VMEM((8, LANES), F32),
            pltpu.VMEM((2 * BLOCKS, LANES), F32),
            pltpu.VMEM((2 * BLOCKS, LANES), F32),
            pltpu.VMEM((2 * BLOCKS, LANES), F32),
            pltpu.VMEM((2 * BLOCKS, LANES), F32),
            pltpu.VMEM((3, NP, 8, LANES), F32),
            pltpu.VMEM((2, BLOCKS, LANES), F32),
            pltpu.VMEM((NZ, BLOCKS, LANES), F32),
            pltpu.VMEM((NZ, 2, LANES), F32),
            pltpu.VMEM((NZ, 2, LANES), F32),
            pltpu.VMEM((8, LANES), F32),
            pltpu.VMEM((8, LANES), F32),
            dma((2, 7)), dma((2, 7)), dma((16,)), dma((16,)), dma((2,)), dma((2,)),
            dma((3, NP)), dma((3, NP)), dma((2, NZ)), dma((2, NZ)), dma((4,)), dma((4,)),
        ],
        compiler_params=pltpu.CompilerParams(
            collective_id=0, has_side_effects=True, vmem_limit_bytes=60 * 1024 * 1024
        ),
        name="sinkhorn",
    )(sources, targets, duals_init.reshape(2, LANES))
    return f.reshape(-1), g.reshape(-1)


def solution(mesh):
    return jax.shard_map(
        body,
        mesh=mesh,
        in_specs=(P("blk", None), P(("blk", "tgt"), None), P(("blk", "tgt"))),
        out_specs=(P("blk"), P(("blk", "tgt"))),
        check_vma=False,
    )
```

time: 237 us -> 80.3 us (0.34)
  blocking collectives: 86.9 us -> 0 us
  Pallas kernels: 0 us -> 77.6 us
  other arithmetic: 55.9 us -> 0 us
  waiting for transfers between devices: 36.6 us -> 0 us
  matrix products: 17.7 us -> 0 us
  starting transfers between devices: 14.6 us -> 0 us
  between operations: 14.3 us -> 0.65 us
  local copies, waits for them, and re-layouts: 10 us -> 1.87 us
    all_to_all x6 -> x0, blocking collectives: 80 us -> none  [the longest x5 67.5 us: sent_to_all(): lax.all_to_all(jnp.broadcast_to(x[None], (count, *x.shape)), axis, 0, 0,...]
    pallas_call x0 -> x1, Pallas kernels: none -> 77.6 us  [body(): pl.pallas_call(functools.partial(kernel, math.log2(n_src), math.log2(n_ds...]
    reduce_sum x8 -> x0, other arithmetic: 31.6 us -> none  [the longest x2 16.1 us: body(): col_part = jnp.sum(jnp.exp(col_scores - col_high[None, :]), axis=0)]
    all_gather x1 -> x0, waiting for transfers between devices: 29.2 us -> none  [all_blocks(): blocks = lax.all_gather(blocks, axes[k])]
    reduce_max x5 -> x0, other arithmetic: 23.3 us -> none  [the longest x2 15.4 us: body(): col_high = over_copies(jnp.max(col_scores, axis=0), BLK)]
    dot_general x1 -> x0, matrix products: 17.7 us -> none  [cost_of(): jnp.dot(left, right.T, preferred_element_type=jnp.float32, precision=lax....]
    all_to_all x2 -> x0, starting transfers between devices: 14.6 us -> none  [the longest x1 9.13 us: sent_to_all(): lax.all_to_all(jnp.broadcast_to(x[None], (count, *x.shape)), axis, 0, 0,...]
    all_to_all x2 -> x0, waiting for transfers between devices: 7.34 us -> none  [the longest x1 7.33 us: sent_and_summed(): blocks = lax.all_to_all(split_up(x, dim, count), axis, 0, 0, tiled=True)]
  transfers between devices with their start and end apart: 3 -> 0, of which waited for: 2 -> 0; matrix products, arithmetic and copies ran while one was open for 3% -> 0% of each run, Pallas kernels for 0% -> 0%
where the time goes in v1:
time: 80.3 us; the launch traced here: 80.1 us
  Pallas kernels  77.6 us (97%)
  local copies, waits for them, and re-layouts  1.87 us (2%)
    pallas_call x1, Pallas kernels, body(): pl.pallas_call(functools.partial(kernel, math.log2(n_src), math.log2(n_ds...  77.6 us
    unnamed x6, local copies, waits for them, and re-layouts  1.87 us

profile of v1, /device:TPU:1, one launch (start us, length us, event | category | flops | bytes accessed | tf_op | source)
XLA Modules:
  0.0 80.1 jit_solution(518455806364082349)
XLA Ops:
  0.6 77.6 %sinkhorn.1 = (f32[8,128]{1,0:T(8,128)}, f32[2,128]{1,0:T(2,128)}) custom-call(f32[1024,128]{1,0:T(8,128)} %src_ref.1, f32[256,128]{1,0:T(8,128)} %tgt_ref.1, f32[2,128]{1,0:T(2,128)} %bitcast.4), custom_call_target="tpu_custom_call" | custom-call | tf_op jit(solution)/shard_map/sinkhorn/pallas_call | solution.py:356
  78.2 0.0 copy-start
  78.2 0.7 copy-done
  78.9 0.0 copy-start.1
  78.9 0.6 copy.7
  79.5 0.0 copy-done.1
  79.5 0.6 copy.8
Async XLA Ops:
  78.2 0.7 copy-start
  78.9 0.6 copy-start.1

commit v2 on v1

v2 whole, which is shorter than its diff:
```python
import functools
import math

import jax
import jax.numpy as jnp
from jax import lax
from jax.experimental import pallas as pl
from jax.experimental.pallas import tpu as pltpu
from jax.sharding import PartitionSpec as P

EPS = 0.05
LOG2E = math.log2(math.e)
SCALE = LOG2E / EPS
MESH = pl.DeviceIdType.MESH
NZ = 8
NP = 16
ROWS = 1024
COLS = 256
BLOCKS = 16
HEAD = 8
D = 128
LANES = 128
CHUNK = 128
CUTS = ((0, HEAD + CHUNK), (HEAD + CHUNK, CHUNK))
F32 = jnp.float32


def lse2(parts):
    high = functools.reduce(jnp.maximum, parts)
    total = functools.reduce(jnp.add, [jnp.exp2(p - high) for p in parts])
    return high + jnp.log2(total)


def kernel(
    log_src, log_dst,
    src_ref, tgt_ref, g0_ref, f_ref, g_ref,
    g0, load_sem, tile, kern, blocks, rows_in, lhs, acc, wide,
    top, row_stat, col_stat, gamma, delta, weight,
    row_buf, pair_buf, z_buf, own_buf, fin_buf, f_own, f_pair,
    ring_send, ring_recv, d2d_send, d2d_recv, x_send, x_recv,
    row_send, row_recv, z_send, z_recv, pair_send, pair_recv,
):
    blk, tgt = lax.axis_index("blk"), lax.axis_index("tgt")
    x_lo, z = blk // NZ, lax.rem(blk, NZ)
    core, x_hi, y = lax.rem(tgt, 2), lax.rem(tgt // 2, 2), tgt // 4
    pair = (blk, tgt + 1 - 2 * core)
    me = x_lo * 8 + tgt // 2

    def on_plane(q):
        return (q // 8) * NZ + z, lax.rem(q, 8) * 2 + core

    def on_ring(other):
        return x_lo * NZ + other, tgt

    def beside(step):
        x = lax.rem(2 * x_hi + x_lo + step + 4, 4)
        return lax.rem(x, 2) * NZ + z, y * 4 + (x // 2) * 2 + x_lo

    swaps = core != x_lo
    left, right = beside(-1), beside(1)
    own = core * NZ + z

    loads = [
        pltpu.make_async_copy(tgt_ref, blocks.at[own, pl.ds(HEAD, COLS), :], load_sem.at[0]),
        pltpu.make_async_copy(g0_ref, g0, load_sem.at[1]),
        pltpu.make_async_copy(src_ref, rows_in, load_sem.at[2]),
    ]
    loads[0].start()
    loads[1].start()

    barrier = pltpu.get_barrier_semaphore()
    for k in range(1, NP):
        pl.semaphore_signal(barrier, inc=1, device_id=on_plane(lax.rem(me + k, NP)), device_id_type=MESH)
    for k in range(1, NZ):
        pl.semaphore_signal(barrier, inc=1, device_id=on_ring(lax.rem(z + k, NZ)), device_id_type=MESH)
    pl.semaphore_signal(barrier, inc=1, device_id=pair, device_id_type=MESH)

    @pl.when(swaps)
    def _():
        for there in (left, right):
            pl.semaphore_signal(barrier, inc=1, device_id=there, device_id_type=MESH)

    @pl.when(jnp.logical_not(swaps))
    def _():
        loads[2].start()

    loads[0].wait()
    loads[1].wait()
    for half in range(2):
        part = blocks[own, HEAD + half * LANES : HEAD + (half + 1) * LANES, :]
        norm = jnp.sum((part * part).T, axis=0, keepdims=True)
        blocks[own, half : half + 1, :] = SCALE * (g0[half : half + 1, :] - norm)

    with jax.named_scope("barrier"):
        pl.semaphore_wait(barrier, NP - 1 + NZ - 1 + 1 + 2 * swaps.astype(jnp.int32))

    def copy(src, dst, send, recv, where):
        return pltpu.make_async_remote_copy(
            src_ref=src, dst_ref=dst, send_sem=send, recv_sem=recv, device_id=where, device_id_type=MESH
        )

    def piece(zb, i):
        start, size = CUTS[i % 2]
        return blocks.at[(NZ if i < 2 else 0) + zb, pl.ds(start, size), :]

    def ring_copy(way, step, i, zb):
        to = on_ring(lax.rem(z + (1 if way == 0 else NZ - 1), NZ))
        slot = 4 * (step - 1) + (i if step < 4 else i % 2)
        return copy(piece(zb, i), piece(zb, i), ring_send.at[way, slot], ring_recv.at[way, slot], to)

    def pair_copy(zb, i):
        return copy(piece(zb, i), piece(zb, i), d2d_send.at[4 * zb + i], d2d_recv.at[4 * zb + i], pair)

    def goes(way, step, i):
        return step < 4 or (way == 0) == (i < 2)

    def swap_copy(side):
        at = pl.ds(side * (ROWS // 2), ROWS // 2)
        return copy(src_ref.at[at, :], rows_in.at[at, :], x_send.at[side], x_recv.at[side], (left, right)[side])

    carrier = core == 1

    @pl.when(jnp.logical_not(carrier))
    def _():
        for i in (2, 3):
            pair_copy(z, i).start()

    @pl.when(carrier)
    def _():
        for i in (0, 1):
            for way in range(2):
                ring_copy(way, 1, i, z).start()
            pair_copy(z, i).start()

    @pl.when(swaps)
    def _():
        for side in range(2):
            swap_copy(side).start()

    @pl.when(carrier)
    def _():
        for i in (2, 3):
            pair_copy(z, i).wait_recv()
            for way in range(2):
                ring_copy(way, 1, i, z).start()

    def origin(way, step):
        return lax.rem(z + (NZ - step if way == 0 else step), NZ)

    def receive(step):
        @pl.when(carrier)
        def _():
            for i in range(4):
                for way in range(2):
                    if goes(way, step, i):
                        zb = origin(way, step)
                        ring_copy(way, step, i, zb).wait_recv()
                        if step < 4 and goes(way, step + 1, i):
                            ring_copy(way, step + 1, i, zb).start()
                        pair_copy(zb, i).start()

    def prepare():
        @pl.when(swaps)
        def _():
            for side in range(2):
                swap_copy(side).wait()

        @pl.when(jnp.logical_not(swaps))
        def _():
            loads[2].wait()

        for r in range(ROWS // LANES):
            rows = rows_in[r * LANES : (r + 1) * LANES, :] * (2 * SCALE)
            high = rows.astype(jnp.bfloat16)
            low = (rows - high.astype(F32)).astype(jnp.bfloat16)
            lhs[r * LANES : (r + 1) * LANES, :] = jnp.concatenate([high, low, high, low], axis=1)
        top[...] = jnp.full_like(top, -jnp.inf)
        acc[...] = jnp.zeros_like(acc)

    def scores(zb):
        outs, heads, at = [], [], []
        for which in (core, 1 - core):
            b = which * NZ + zb
            t = blocks[b, HEAD:, :]
            high = t.astype(jnp.bfloat16)
            low = (t - high.astype(F32)).astype(jnp.bfloat16)
            rhs = jnp.concatenate([high, high, low, low], axis=1)
            outs.append(lax.dot_general(lhs[...], rhs, (((1,), (1,)), ((), ())), preferred_element_type=F32))
            heads += [jnp.broadcast_to(blocks[b, h : h + 1, :], (8, LANES)) for h in range(2)]
            at.append(b)
        for k in range(0, ROWS, 8):
            rows = slice(k, k + 8)
            parts = []
            for c in range(4):
                cut = slice((c % 2) * LANES, (c % 2 + 1) * LANES)
                parts.append(outs[c // 2][rows, cut] + heads[c])
                tile[at[c // 2], rows, cut] = parts[c]
            old = top[rows, :]
            new = jnp.maximum(jnp.maximum(parts[0], parts[1]), jnp.maximum(parts[2], parts[3]))
            new = jnp.maximum(old, new)
            top[rows, :] = new
            e = [jnp.exp2(p - new) for p in parts]
            acc[rows, :] = acc[rows, :] * jnp.exp2(old - new) + ((e[0] + e[1]) + (e[2] + e[3]))

    def scores_at(zb):
        @pl.when(jnp.logical_not(carrier))
        def _():
            for i in range(4):
                pair_copy(zb, i).wait_recv()

        scores(zb)

    def scores_beside(step):
        def one(i, carry):
            scores_at(lax.rem(z + jnp.where(i == 0, NZ - step, step), NZ))
            return carry

        lax.fori_loop(0, 2, one, 0)

    with jax.named_scope("receive_1"):
        receive(1)
    with jax.named_scope("prepare"):
        prepare()
    with jax.named_scope("scores_0"):
        @pl.when(jnp.logical_not(carrier))
        def _():
            for i in range(2):
                pair_copy(z, i).wait_recv()

        scores(z)
    with jax.named_scope("receive_2"):
        receive(2)
    with jax.named_scope("scores_1"):
        scores_beside(1)
    with jax.named_scope("receive_3"):
        receive(3)
    with jax.named_scope("scores_2"):
        scores_beside(2)
    with jax.named_scope("receive_4"):
        receive(4)
    with jax.named_scope("scores_3"):
        scores_beside(3)
    with jax.named_scope("scores_4"):
        scores_at(lax.rem(z + 4, NZ))

    def spread(row):
        for r in range(ROWS // LANES):
            wide[r * LANES : (r + 1) * LANES, :] = jnp.broadcast_to(row[r : r + 1, :], (LANES, LANES)).T

    def across_plane(phase):
        def send(k, carry):
            q = lax.rem(me + k, NP)
            slot = row_buf.at[phase, me]
            copy(slot, slot, row_send.at[phase, k], row_recv.at[phase, me], on_plane(q)).start()
            return carry

        lax.fori_loop(1, NP, send, 0)

        def arrive(k, carry):
            q = lax.rem(me + k, NP)
            slot = row_buf.at[phase, q]
            copy(slot, slot, row_send.at[phase, k], row_recv.at[phase, q], on_plane(q)).wait_recv()
            return carry

        lax.fori_loop(1, NP, arrive, 0)

    def tree(op, xs):
        while len(xs) > 1:
            xs = [op(*xs[i : i + 2]) if i + 1 < len(xs) else xs[i] for i in range(0, len(xs), 2)]
        return xs[0]

    QUAD = 4
    TALL = 256

    def quads(core_of):
        return [core_of * NZ + q * QUAD for q in range(NZ // QUAD)]

    def pick(x, k, h):
        return x[8 * k : 8 * k + 8, h * LANES : (h + 1) * LANES]

    def summed(op, xs):
        return op(functools.reduce(op, xs[0::2]), functools.reduce(op, xs[1::2])) if len(xs) > 1 else xs[0]

    def column_pass(first, into, held, term, op, start):
        def some(r, total):
            at = pl.ds(pl.multiple_of(r * TALL, TALL), TALL)
            w = wide.at[at, :]
            result = []
            for q in range(QUAD):
                view = held.at[first + q, at, :]
                for h in range(2):
                    xs = [term(pick(view, k, h), w[8 * k : 8 * k + 8, :]) for k in range(TALL // 8)]
                    result.append(op(total[2 * q + h], summed(op, xs)))
            return tuple(result)

        total = lax.fori_loop(0, ROWS // TALL, some, (jnp.full((8, LANES), start, F32),) * (2 * QUAD))
        fold = jnp.max if op is jnp.maximum else jnp.sum
        for c in range(2 * QUAD):
            into[pl.ds(2 * first + c, 1), :] = fold(total[c], axis=0, keepdims=True)

    def exp_pass(first):
        tall = 128

        def some(r, total):
            at = pl.ds(pl.multiple_of(r * tall, tall), tall)
            w = wide[at, :]
            result = []
            for q in range(QUAD):
                view = tile.at[first + q, at, :]
                out = kern.at[first + q, at, :]
                for h in range(2):
                    low = gamma[pl.ds(2 * (first + q) + h, 1), :]
                    entry = jnp.exp2((view[:, h * LANES : (h + 1) * LANES] + w) - low)
                    out[:, h * LANES : (h + 1) * LANES] = entry
                    result.append(total[2 * q + h] + jnp.sum(entry.reshape(tall // 8, 8, LANES), axis=0))
            return tuple(result)

        total = lax.fori_loop(0, ROWS // tall, some, (jnp.zeros((8, LANES), F32),) * (2 * QUAD))
        for c in range(2 * QUAD):
            col_stat[pl.ds(2 * first + c, 1), :] = jnp.sum(total[c], axis=0, keepdims=True)

    def row_pass(first, fresh):
        v = [weight[pl.ds(2 * first + c, 1), :] for c in range(2 * QUAD)]

        def some(r, carry):
            at = pl.ds(pl.multiple_of(r * TALL, TALL), TALL)
            views = [kern.at[first + q, at, :] for q in range(QUAD)]
            out = acc.at[at, :]
            for k in range(TALL // 8):
                total = summed(jnp.add, [pick(views[c // 2], k, c % 2) * v[c] for c in range(2 * QUAD)])
                out[8 * k : 8 * k + 8, :] = total if fresh else out[8 * k : 8 * k + 8, :] + total
            return carry

        lax.fori_loop(0, ROWS // TALL, some, 0)

    def halves(step):
        return pl.ds(pl.multiple_of(step * BLOCKS, BLOCKS), BLOCKS)

    def log_sums(core_of):
        rows = halves(core_of)
        col_stat[rows, :] = gamma[rows, :] + jnp.log2(col_stat[rows, :])

    def with_pair(phase, columns):
        for first in quads(1 - core):
            columns(first)
        log_sums(1 - core)
        rows = halves(1 - core)
        swap = copy(col_stat.at[rows, :], pair_buf.at[phase], pair_send.at[phase], pair_recv.at[phase], pair)
        swap.start()
        for first in quads(core):
            columns(first)
        log_sums(core)
        swap.wait()
        return lse2([col_stat[halves(core), :], pair_buf[phase]])

    def round_ring(phase, src, dst):
        def send(k, carry):
            other = lax.rem(z + k, NZ)
            copy(src(other), dst(z), z_send.at[phase, k], z_recv.at[phase, z], on_ring(other)).start()
            return carry

        lax.fori_loop(1, NZ, send, 0)

        def arrive(k, carry):
            other = lax.rem(z + k, NZ)
            copy(src(other), dst(other), z_send.at[phase, k], z_recv.at[phase, other], on_ring(other)).wait_recv()
            return carry

        lax.fori_loop(1, NZ, arrive, 0)

    with jax.named_scope("row_lse"):
        for r in range(ROWS // LANES):
            at = slice(r * LANES, (r + 1) * LANES)
            lane_top = top[at, :].T
            high = jnp.max(lane_top, axis=0, keepdims=True)
            total = jnp.sum(acc[at, :].T * jnp.exp2(lane_top - high), axis=0, keepdims=True)
            row_buf[0, me, r : r + 1, :] = high + jnp.log2(total)
    with jax.named_scope("plane_0"):
        across_plane(0)
    with jax.named_scope("spread"):
        phi = -log_dst - lse2([row_buf[0, q] for q in range(NP)])
        spread(phi)
    with jax.named_scope("gamma"):
        for which in range(2):
            for first in quads(which):
                column_pass(first, gamma, tile, jnp.add, jnp.maximum, -jnp.inf)
    with jax.named_scope("exp"):
        z_buf[z] = with_pair(0, exp_pass)
    with jax.named_scope("ring_0"):
        round_ring(0, lambda other: z_buf.at[z], lambda other: z_buf.at[other])
    delta[halves(core), :] = -log_src - lse2([z_buf[k] for k in range(NZ)])
    half = delta.at[halves(core), :]
    give = copy(half, half, pair_send.at[2], pair_recv.at[2], pair)
    give.start()

    def weigh(core_of):
        rows = halves(core_of)
        weight[rows, :] = jnp.exp2(delta[rows, :] + gamma[rows, :])

    with jax.named_scope("rows_own"):
        weigh(core)
        for n, first in enumerate(quads(core)):
            row_pass(first, n == 0)
    with jax.named_scope("give"):
        give.wait()
    with jax.named_scope("rows_pair"):
        weigh(1 - core)
        for first in quads(1 - core):
            row_pass(first, False)
        for r in range(ROWS // LANES):
            at = slice(r * LANES, (r + 1) * LANES)
            row_buf[1, me, r : r + 1, :] = jnp.sum(acc[at, :].T, axis=0, keepdims=True)
    with jax.named_scope("plane_1"):
        across_plane(1)
    with jax.named_scope("spread"):
        log_sum = log_dst + jnp.log2(jnp.sum(row_buf[1], axis=0))
        spread(jnp.exp2(-log_sum))
    with jax.named_scope("f"):
        for r in range(ROWS // LANES):
            rows = rows_in[r * LANES : (r + 1) * LANES, :]
            row_stat[r : r + 1, :] = jnp.sum((rows * rows).T, axis=0, keepdims=True)
        f_own[...] = row_stat[...] + (phi - log_sum) / SCALE

    hand = copy(f_own, f_pair, pair_send.at[3], pair_recv.at[3], pair)
    hand.start()
    with jax.named_scope("cols"):
        joined = with_pair(1, lambda first: column_pass(first, col_stat, kern, jnp.multiply, jnp.add, 0.0))
    for k in range(NZ):
        own_buf[k] = joined[2 * k : 2 * k + 2, :]
    fin_buf[z] = own_buf[z]
    with jax.named_scope("ring_1"):
        round_ring(1, lambda other: own_buf.at[other], lambda other: fin_buf.at[other])
    g_ref[...] = g0[...] - (log_src + lse2([fin_buf[k] for k in range(NZ)])) / SCALE
    hand.wait()
    f_ref[...] = jnp.where(swaps, f_pair[...], f_own[...])

    @pl.when(carrier)
    def _():
        for step in range(1, 5):
            for i in range(4):
                for way in range(2):
                    if goes(way, step, i):
                        ring_copy(way, step, i, z).wait_send()
        for i in range(2):
            pair_copy(z, i).wait_send()
        for step in range(1, 5):
            for way in range(2):
                for i in range(4):
                    if goes(way, step, i):
                        pair_copy(origin(way, step), i).wait_send()

    @pl.when(jnp.logical_not(carrier))
    def _():
        for i in (2, 3):
            pair_copy(z, i).wait_send()

    for phase in range(2):
        def left_row(k, carry):
            slot = row_buf.at[phase, me]
            copy(slot, slot, row_send.at[phase, k], row_recv.at[phase, me], pair).wait_send()
            return carry

        lax.fori_loop(1, NP, left_row, 0)
    for phase in range(2):
        def left_ring(k, carry):
            src = z_buf.at[z] if phase == 0 else own_buf.at[z]
            copy(src, src, z_send.at[phase, k], z_recv.at[phase, z], on_ring(z)).wait_send()
            return carry

        lax.fori_loop(1, NZ, left_ring, 0)


def body(sources, targets, duals_init):
    n_src = sources.shape[0] * lax.axis_size("blk")
    n_dst = targets.shape[0] * lax.axis_size("blk") * lax.axis_size("tgt")
    vmem = pl.BlockSpec(memory_space=pltpu.VMEM)
    dma = pltpu.SemaphoreType.DMA
    f, g = pl.pallas_call(
        functools.partial(kernel, math.log2(n_src), math.log2(n_dst)),
        out_shape=(jax.ShapeDtypeStruct((8, LANES), F32), jax.ShapeDtypeStruct((2, LANES), F32)),
        in_specs=[pl.BlockSpec(memory_space=pl.ANY)] * 3,
        out_specs=(vmem, vmem),
        scratch_shapes=[
            pltpu.VMEM((2, LANES), F32),
            dma((3,)),
            pltpu.VMEM((BLOCKS, ROWS, COLS), F32),
            pltpu.VMEM((BLOCKS, ROWS, COLS), F32),
            pltpu.VMEM((BLOCKS, HEAD + COLS, D), F32),
            pltpu.VMEM((ROWS, D), F32),
            pltpu.VMEM((ROWS, 4 * D), jnp.bfloat16),
            pltpu.VMEM((ROWS, LANES), F32),
            pltpu.VMEM((ROWS, LANES), F32),
            pltpu.VMEM((ROWS, LANES), F32),
            pltpu.VMEM((8, LANES), F32),
            pltpu.VMEM((2 * BLOCKS, LANES), F32),
            pltpu.VMEM((2 * BLOCKS, LANES), F32),
            pltpu.VMEM((2 * BLOCKS, LANES), F32),
            pltpu.VMEM((2 * BLOCKS, LANES), F32),
            pltpu.VMEM((2, NP, 8, LANES), F32),
            pltpu.VMEM((2, BLOCKS, LANES), F32),
            pltpu.VMEM((NZ, BLOCKS, LANES), F32),
            pltpu.VMEM((NZ, 2, LANES), F32),
            pltpu.VMEM((NZ, 2, LANES), F32),
            pltpu.VMEM((8, LANES), F32),
            pltpu.VMEM((8, LANES), F32),
            dma((2, 14)), dma((2, 14)), dma((32,)), dma((32,)), dma((2,)), dma((2,)),
            dma((2, NP)), dma((2, NP)), dma((2, NZ)), dma((2, NZ)), dma((4,)), dma((4,)),
        ],
        compiler_params=pltpu.CompilerParams(
            collective_id=0, has_side_effects=True, vmem_limit_bytes=60 * 1024 * 1024
        ),
        name="sinkhorn",
    )(sources, targets, duals_init.reshape(2, LANES))
    return f.reshape(-1), g.reshape(-1)


def solution(mesh):
    return jax.shard_map(
        body,
        mesh=mesh,
        in_specs=(P("blk", None), P(("blk", "tgt"), None), P(("blk", "tgt"))),
        out_specs=(P("blk"), P(("blk", "tgt"))),
        check_vma=False,
    )
```

time: 80.3 us -> 59.9 us (0.75)
  Pallas kernels: 77.6 us -> 57.3 us
    pallas_call x1, Pallas kernels: 77.6 us -> 57.3 us  [body(): pl.pallas_call(functools.partial(kernel, math.log2(n_src), math.log2(n_ds...]
where the time goes in v2:
time: 59.9 us; the launch traced here: 59.8 us
  Pallas kernels  57.3 us (96%)
  local copies, waits for them, and re-layouts  1.87 us (3%)
  between operations  0.65 us (1%)
    pallas_call x1, Pallas kernels, body(): pl.pallas_call(functools.partial(kernel, math.log2(n_src), math.log2(n_ds...  57.3 us
    unnamed x6, local copies, waits for them, and re-layouts  1.87 us

profile of v2, /device:TPU:1, one launch (start us, length us, event | category | flops | bytes accessed | tf_op | source)
XLA Modules:
  0.0 59.8 jit_solution(14591938196149477398)
XLA Ops:
  0.6 57.3 %sinkhorn.1 = (f32[8,128]{1,0:T(8,128)}, f32[2,128]{1,0:T(2,128)}) custom-call(f32[1024,128]{1,0:T(8,128)} %src_ref.1, f32[256,128]{1,0:T(8,128)} %tgt_ref.1, f32[2,128]{1,0:T(2,128)} %bitcast.4), custom_call_target="tpu_custom_call" | custom-call | tf_op jit(solution)/shard_map/sinkhorn/pallas_call | solution.py:478
  57.9 0.0 copy-start
  57.9 0.7 %copy-done = f32[8,128]{1,0:T(8,128)S(1)} copy-done((f32[8,128]{1,0:T(8,128)S(1)}, f32[8,128]{1,0:T(8,128)}, u32[]{:S(2)}) %copy-start) | copy-done | bytes 4120
  58.6 0.0 copy-start.1
  58.6 0.6 copy.7
  59.2 0.0 copy-done.1
  59.2 0.6 copy.8
Async XLA Ops:
  57.9 0.7 %copy-start = (f32[8,128]{1,0:T(8,128)S(1)}, f32[8,128]{1,0:T(8,128)}, u32[]{:S(2)}) copy-start(f32[8,128]{1,0:T(8,128)} %get-tuple-element.4) | copy-start | bytes 12292
  58.6 0.6 %copy-start.1 = (f32[2,128]{1,0:T(2,128)S(1)}, f32[2,128]{1,0:T(2,128)}, u32[]{:S(2)}) copy-start(f32[2,128]{1,0:T(2,128)} %get-tuple-element.5) | copy-start | bytes 3076

commit v3 on v2

--- a/solution.py
+++ b/solution.py
@@ -147,17 +147,37 @@
     def origin(way, step):
         return lax.rem(z + (NZ - step if way == 0 else step), NZ)
 
-    def receive(step):
+    def receive(step, half):
         @pl.when(carrier)
         def _():
+            for i in range(2):
+                start, size = CUTS[i]
+                for way in range(2):
+                    zb = origin(way, step)
+                    part = blocks.at[(1 - half) * NZ + zb, pl.ds(start, size), :]
+                    to = on_ring(lax.rem(z + (1 if way == 0 else NZ - 1), NZ))
+                    slot = 4 * (step - 1) + 2 * half + i
+                    came = copy(part, part, ring_send.at[way, slot], ring_recv.at[way, slot], to)
+                    came.wait_recv()
+                    last = step == 3
+                    far = 12 + i
+                    slot = jnp.where(last, far, slot + 4)
+
+                    @pl.when(jnp.logical_or(jnp.logical_not(last), (half == 0) == (way == 0)))
+                    def _():
+                        copy(part, part, ring_send.at[way, slot], ring_recv.at[way, slot], to).start()
+
+                    at = 4 * zb + 2 * half + i
+                    copy(part, part, d2d_send.at[at], d2d_recv.at[at], pair).start()
+
+    def receive_far():
+        @pl.when(carrier)
+        def _():
             for i in range(4):
-                for way in range(2):
-                    if goes(way, step, i):
-                        zb = origin(way, step)
-                        ring_copy(way, step, i, zb).wait_recv()
-                        if step < 4 and goes(way, step + 1, i):
-                            ring_copy(way, step + 1, i, zb).start()
-                        pair_copy(zb, i).start()
+                way = 0 if i < 2 else 1
+                zb = origin(way, 4)
+                ring_copy(way, 4, i, zb).wait_recv()
+                pair_copy(zb, i).start()
 
     def prepare():
         @pl.when(swaps)
@@ -202,72 +222,78 @@
             e = [jnp.exp2(p - new) for p in parts]
             acc[rows, :] = acc[rows, :] * jnp.exp2(old - new) + ((e[0] + e[1]) + (e[2] + e[3]))
 
-    def scores_at(zb):
+    def scores_step(n, carry):
+        step = n // 2 + 1
+        half = lax.rem(n, 2)
+
+        @pl.when(jnp.logical_and(n >= 2, n < 6))
+        def _():
+            receive(step, half)
+
+        @pl.when(n == 2 * NZ // 2)
+        def _():
+            receive_far()
+
+        off = n // 2
+        zb = lax.rem(z + jnp.where(half == 0, NZ - off, off), NZ)
+
         @pl.when(jnp.logical_not(carrier))
         def _():
-            for i in range(4):
+            for i in range(2):
                 pair_copy(zb, i).wait_recv()
 
+            @pl.when(n > 1)
+            def _():
+                for i in (2, 3):
+                    pair_copy(zb, i).wait_recv()
+
         scores(zb)
-
-    def scores_beside(step):
-        def one(i, carry):
-            scores_at(lax.rem(z + jnp.where(i == 0, NZ - step, step), NZ))
-            return carry
-
-        lax.fori_loop(0, 2, one, 0)
+        return carry
 
     with jax.named_scope("receive_1"):
-        receive(1)
+        receive(1, 0)
+        receive(1, 1)
     with jax.named_scope("prepare"):
         prepare()
-    with jax.named_scope("scores_0"):
-        @pl.when(jnp.logical_not(carrier))
-        def _():
-            for i in range(2):
-                pair_copy(z, i).wait_recv()
-
-        scores(z)
-    with jax.named_scope("receive_2"):
-        receive(2)
-    with jax.named_scope("scores_1"):
-        scores_beside(1)
-    with jax.named_scope("receive_3"):
-        receive(3)
-    with jax.named_scope("scores_2"):
-        scores_beside(2)
-    with jax.named_scope("receive_4"):
-        receive(4)
-    with jax.named_scope("scores_3"):
-        scores_beside(3)
-    with jax.named_scope("scores_4"):
-        scores_at(lax.rem(z + 4, NZ))
+    with jax.named_scope("scores"):
+        lax.fori_loop(1, NZ + 1, scores_step, 0)
 
     def spread(row):
         for r in range(ROWS // LANES):
             wide[r * LANES : (r + 1) * LANES, :] = jnp.broadcast_to(row[r : r + 1, :], (LANES, LANES)).T
 
-    def across_plane(phase):
-        def send(k, carry):
-            q = lax.rem(me + k, NP)
-            slot = row_buf.at[phase, me]
-            copy(slot, slot, row_send.at[phase, k], row_recv.at[phase, me], on_plane(q)).start()
-            return carry
-
-        lax.fori_loop(1, NP, send, 0)
+    x_at = 2 * x_hi + x_lo
+
+    def off_plane(dx, dy):
+        x, row = lax.rem(x_at + dx, 4), lax.rem(y + dy, 4)
+        return lax.rem(x, 2) * NZ + z, row * 4 + (x // 2) * 2 + core
+
+    def plane_copies(phase):
+        slot = row_buf.at[phase, me]
+        ways = sorted(
+            ((dx, dy) for dx in range(4) for dy in range(4) if dx or dy),
+            key=lambda d: -min(d[0], 4 - d[0]) - min(d[1], 4 - d[1]),
+        )
+        return [
+            copy(slot, slot, row_send.at[phase, k], row_recv.at[phase, me], off_plane(*d)) for k, d in enumerate(ways)
+        ]
+
+    def across_plane(phase, meanwhile):
+        for c in plane_copies(phase):
+            c.start()
+        meanwhile()
 
         def arrive(k, carry):
             q = lax.rem(me + k, NP)
             slot = row_buf.at[phase, q]
-            copy(slot, slot, row_send.at[phase, k], row_recv.at[phase, q], on_plane(q)).wait_recv()
+            copy(slot, slot, row_send.at[phase, 0], row_recv.at[phase, q], pair).wait_recv()
             return carry
 
         lax.fori_loop(1, NP, arrive, 0)
 
-    def tree(op, xs):
-        while len(xs) > 1:
-            xs = [op(*xs[i : i + 2]) if i + 1 < len(xs) else xs[i] for i in range(0, len(xs), 2)]
-        return xs[0]
+    def plane_sent(phase):
+        for c in plane_copies(phase):
+            c.wait_send()
 
     QUAD = 4
     TALL = 256
@@ -299,7 +325,7 @@
             into[pl.ds(2 * first + c, 1), :] = fold(total[c], axis=0, keepdims=True)
 
     def exp_pass(first):
-        tall = 128
+        tall = 256
 
         def some(r, total):
             at = pl.ds(pl.multiple_of(r * tall, tall), tall)
@@ -336,34 +362,38 @@
     def halves(step):
         return pl.ds(pl.multiple_of(step * BLOCKS, BLOCKS), BLOCKS)
 
-    def log_sums(core_of):
-        rows = halves(core_of)
-        col_stat[rows, :] = gamma[rows, :] + jnp.log2(col_stat[rows, :])
-
-    def with_pair(phase, columns):
-        for first in quads(1 - core):
+    def quad_rows(first):
+        return pl.ds(pl.multiple_of(2 * first, 8), 8)
+
+    def with_pair(phase, columns, emit):
+        swaps_out = []
+        for q, first in enumerate(quads(1 - core)):
             columns(first)
-        log_sums(1 - core)
-        rows = halves(1 - core)
-        swap = copy(col_stat.at[rows, :], pair_buf.at[phase], pair_send.at[phase], pair_recv.at[phase], pair)
-        swap.start()
-        for first in quads(core):
+            rows = quad_rows(first)
+            col_stat[rows, :] = gamma[rows, :] + jnp.log2(col_stat[rows, :])
+            to = pair_buf.at[phase, pl.ds(8 * q, 8), :]
+            k = 2 * phase + q
+            swaps_out.append(copy(col_stat.at[rows, :], to, pair_send.at[k], pair_recv.at[k], pair))
+            swaps_out[q].start()
+        for q, first in enumerate(quads(core)):
             columns(first)
-        log_sums(core)
-        swap.wait()
-        return lse2([col_stat[halves(core), :], pair_buf[phase]])
-
-    def round_ring(phase, src, dst):
-        def send(k, carry):
-            other = lax.rem(z + k, NZ)
-            copy(src(other), dst(z), z_send.at[phase, k], z_recv.at[phase, z], on_ring(other)).start()
-            return carry
-
-        lax.fori_loop(1, NZ, send, 0)
-
+            rows = quad_rows(first)
+            part = gamma[rows, :] + jnp.log2(col_stat[rows, :])
+            swaps_out[q].wait()
+            emit(q, lse2([part, pair_buf[phase, 8 * q : 8 * q + 8, :]]))
+
+    def ring_copies(q):
+        part = z_buf.at[z, pl.ds(8 * q, 8), :]
+        return [
+            copy(part, part, z_send.at[q, k], z_recv.at[q, z], on_ring(lax.rem(z + k, NZ))) for k in (4, 3, 5, 2, 6, 1, 7)
+        ]
+
+    def ring_waits(slots):
         def arrive(k, carry):
             other = lax.rem(z + k, NZ)
-            copy(src(other), dst(other), z_send.at[phase, k], z_recv.at[phase, other], on_ring(other)).wait_recv()
+            for phase, ref in slots:
+                part = ref(other)
+                copy(part, part, z_send.at[phase, 0], z_recv.at[phase, other], pair).wait_recv()
             return carry
 
         lax.fori_loop(1, NZ, arrive, 0)
@@ -375,22 +405,50 @@
             high = jnp.max(lane_top, axis=0, keepdims=True)
             total = jnp.sum(acc[at, :].T * jnp.exp2(lane_top - high), axis=0, keepdims=True)
             row_buf[0, me, r : r + 1, :] = high + jnp.log2(total)
+
+    def after_gather():
+        for r in range(ROWS // LANES):
+            rows = rows_in[r * LANES : (r + 1) * LANES, :]
+            row_stat[r : r + 1, :] = jnp.sum((rows * rows).T, axis=0, keepdims=True)
+
+        @pl.when(carrier)
+        def _():
+            for step in range(1, 5):
+                for i in range(4):
+                    for way in range(2):
+                        if goes(way, step, i):
+                            ring_copy(way, step, i, z).wait_send()
+                            pair_copy(origin(way, step), i).wait_send()
+            for i in range(2):
+                pair_copy(z, i).wait_send()
+
+        @pl.when(jnp.logical_not(carrier))
+        def _():
+            for i in (2, 3):
+                pair_copy(z, i).wait_send()
+
     with jax.named_scope("plane_0"):
-        across_plane(0)
+        across_plane(0, after_gather)
     with jax.named_scope("spread"):
         phi = -log_dst - lse2([row_buf[0, q] for q in range(NP)])
         spread(phi)
-    with jax.named_scope("gamma"):
-        for which in range(2):
-            for first in quads(which):
-                column_pass(first, gamma, tile, jnp.add, jnp.maximum, -jnp.inf)
+
+    def first_columns(first):
+        column_pass(first, gamma, tile, jnp.add, jnp.maximum, -jnp.inf)
+        exp_pass(first)
+
+    def to_ring(q, joined):
+        z_buf[z, 8 * q : 8 * q + 8, :] = joined
+        for c in ring_copies(q):
+            c.start()
+
     with jax.named_scope("exp"):
-        z_buf[z] = with_pair(0, exp_pass)
+        with_pair(0, first_columns, to_ring)
     with jax.named_scope("ring_0"):
-        round_ring(0, lambda other: z_buf.at[z], lambda other: z_buf.at[other])
+        ring_waits([(q, lambda other, q=q: z_buf.at[other, pl.ds(8 * q, 8), :]) for q in range(2)])
     delta[halves(core), :] = -log_src - lse2([z_buf[k] for k in range(NZ)])
     half = delta.at[halves(core), :]
-    give = copy(half, half, pair_send.at[2], pair_recv.at[2], pair)
+    give = copy(half, half, pair_send.at[4], pair_recv.at[4], pair)
     give.start()
 
     def weigh(core_of):
@@ -410,64 +468,52 @@
         for r in range(ROWS // LANES):
             at = slice(r * LANES, (r + 1) * LANES)
             row_buf[1, me, r : r + 1, :] = jnp.sum(acc[at, :].T, axis=0, keepdims=True)
+
+    def after_ring():
+        plane_sent(0)
+        for q in range(2):
+            for c in ring_copies(q):
+                c.wait_send()
+
     with jax.named_scope("plane_1"):
-        across_plane(1)
+        across_plane(1, after_ring)
     with jax.named_scope("spread"):
         log_sum = log_dst + jnp.log2(jnp.sum(row_buf[1], axis=0))
         spread(jnp.exp2(-log_sum))
-    with jax.named_scope("f"):
-        for r in range(ROWS // LANES):
-            rows = rows_in[r * LANES : (r + 1) * LANES, :]
-            row_stat[r : r + 1, :] = jnp.sum((rows * rows).T, axis=0, keepdims=True)
         f_own[...] = row_stat[...] + (phi - log_sum) / SCALE
-
-    hand = copy(f_own, f_pair, pair_send.at[3], pair_recv.at[3], pair)
+    hand = copy(f_own, f_pair, pair_send.at[5], pair_recv.at[5], pair)
     hand.start()
+
+    def part_copy(to):
+        return copy(own_buf.at[to], fin_buf.at[z], z_send.at[2, to], z_recv.at[2, z], on_ring(to))
+
+    def to_owners(q, joined):
+        for i in range(NZ // 2):
+            to = NZ // 2 * q + i
+            part = joined[2 * i : 2 * i + 2, :]
+            own_buf[to] = part
+
+            @pl.when(z == to)
+            def _():
+                fin_buf[to] = part
+
+            @pl.when(z != to)
+            def _():
+                part_copy(to).start()
+
     with jax.named_scope("cols"):
-        joined = with_pair(1, lambda first: column_pass(first, col_stat, kern, jnp.multiply, jnp.add, 0.0))
-    for k in range(NZ):
-        own_buf[k] = joined[2 * k : 2 * k + 2, :]
-    fin_buf[z] = own_buf[z]
+        with_pair(1, lambda first: column_pass(first, col_stat, kern, jnp.multiply, jnp.add, 0.0), to_owners)
     with jax.named_scope("ring_1"):
-        round_ring(1, lambda other: own_buf.at[other], lambda other: fin_buf.at[other])
+        plane_sent(1)
+        hand.wait()
+        f_ref[...] = jnp.where(swaps, f_pair[...], f_own[...])
+        ring_waits([(2, lambda other: fin_buf.at[other])])
     g_ref[...] = g0[...] - (log_src + lse2([fin_buf[k] for k in range(NZ)])) / SCALE
-    hand.wait()
-    f_ref[...] = jnp.where(swaps, f_pair[...], f_own[...])
-
-    @pl.when(carrier)
-    def _():
-        for step in range(1, 5):
-            for i in range(4):
-                for way in range(2):
-                    if goes(way, step, i):
-                        ring_copy(way, step, i, z).wait_send()
-        for i in range(2):
-            pair_copy(z, i).wait_send()
-        for step in range(1, 5):
-            for way in range(2):
-                for i in range(4):
-                    if goes(way, step, i):
-                        pair_copy(origin(way, step), i).wait_send()
-
-    @pl.when(jnp.logical_not(carrier))
-    def _():
-        for i in (2, 3):
-            pair_copy(z, i).wait_send()
-
-    for phase in range(2):
-        def left_row(k, carry):
-            slot = row_buf.at[phase, me]
-            copy(slot, slot, row_send.at[phase, k], row_recv.at[phase, me], pair).wait_send()
-            return carry
-
-        lax.fori_loop(1, NP, left_row, 0)
-    for phase in range(2):
-        def left_ring(k, carry):
-            src = z_buf.at[z] if phase == 0 else own_buf.at[z]
-            copy(src, src, z_send.at[phase, k], z_recv.at[phase, z], on_ring(z)).wait_send()
-            return carry
-
-        lax.fori_loop(1, NZ, left_ring, 0)
+    for to in range(NZ):
+
+        @pl.when(z != to)
+        def _():
+            part_copy(to).wait_send()
 
 
 def body(sources, targets, duals_init):
@@ -477,7 +523,7 @@
     dma = pltpu.SemaphoreType.DMA
     f, g = pl.pallas_call(
         functools.partial(kernel, math.log2(n_src), math.log2(n_dst)),
-        out_shape=(jax.ShapeDtypeStruct((8, LANES), F32), jax.ShapeDtypeStruct((2, LANES), F32)),
+        out_shape=(pltpu.VMEM((8, LANES), F32), pltpu.VMEM((2, LANES), F32)),
         in_specs=[pl.BlockSpec(memory_space=pl.ANY)] * 3,
         out_specs=(vmem, vmem),
         scratch_shapes=[
@@ -504,7 +550,7 @@
             pltpu.VMEM((8, LANES), F32),
             pltpu.VMEM((8, LANES), F32),
             dma((2, 14)), dma((2, 14)), dma((32,)), dma((32,)), dma((2,)), dma((2,)),
-            dma((2, NP)), dma((2, NP)), dma((2, NZ)), dma((2, NZ)), dma((4,)), dma((4,)),
+            dma((2, NP)), dma((2, NP)), dma((3, NZ)), dma((3, NZ)), dma((6,)), dma((6,)),
         ],
         compiler_params=pltpu.CompilerParams(
             collective_id=0, has_side_effects=True, vmem_limit_bytes=60 * 1024 * 1024

time: 59.9 us -> 57.6 us (0.962)
  Pallas kernels: 57.3 us -> 55.7 us
  local copies, waits for them, and re-layouts: 1.87 us -> 1.16 us
    pallas_call x1, Pallas kernels: 57.3 us -> 55.7 us  [body(): pl.pallas_call(functools.partial(kernel, math.log2(n_src), math.log2(n_ds...]
    unnamed x6 -> x2, local copies, waits for them, and re-layouts: 1.87 us -> 1.16 us
where the time goes in v3:
time: 57.6 us; the launch traced here: 57.5 us
  Pallas kernels  55.7 us (97%)
  local copies, waits for them, and re-layouts  1.16 us (2%)
  between operations  0.64 us (1%)
    pallas_call x1, Pallas kernels, body(): pl.pallas_call(functools.partial(kernel, math.log2(n_src), math.log2(n_ds...  55.7 us
    unnamed x2, local copies, waits for them, and re-layouts  1.16 us

profile of v3, /device:TPU:1, one launch (start us, length us, event | category | flops | bytes accessed | tf_op | source)
XLA Modules:
  0.0 57.5 jit_solution(14998008822456470898)
XLA Ops:
  0.6 55.7 %sinkhorn.1 = (f32[8,128]{1,0:T(8,128)S(1)}, f32[2,128]{1,0:T(2,128)S(1)}) custom-call(f32[1024,128]{1,0:T(8,128)} %src_ref.1, f32[256,128]{1,0:T(8,128)} %tgt_ref.1, f32[2,128]{1,0:T(2,128)} %bitcast.5), custom_call_target="tpu_custom_call" | custom-call | tf_op jit(solution)/shard_map/sinkhorn/pallas_call | solution.py:524
  56.4 0.6 %copy.7 = f32[1024]{0:T(1024)} copy(f32[1024]{0:T(1024)S(1)} %bitcast.3) | data formatting | bytes 8192
  57.0 0.6 copy.8

commit v4 on v3

--- a/solution.py
+++ b/solution.py
@@ -106,10 +106,14 @@
     def ring_copy(way, step, i, zb):
         to = on_ring(lax.rem(z + (1 if way == 0 else NZ - 1), NZ))
         slot = 4 * (step - 1) + (i if step < 4 else i % 2)
-        return copy(piece(zb, i), piece(zb, i), ring_send.at[way, slot], ring_recv.at[way, slot], to)
-
-    def pair_copy(zb, i):
-        return copy(piece(zb, i), piece(zb, i), d2d_send.at[4 * zb + i], d2d_recv.at[4 * zb + i], pair)
+        return copy(piece(zb, i), piece(zb, i), ring_send, ring_recv.at[way, slot], to)
+
+    def pair_copy(zb, of):
+        whole = blocks.at[of * NZ + zb]
+        return copy(whole, whole, d2d_send, d2d_recv.at[zb], pair)
+
+    def bytes_of(ref, send, recv):
+        return copy(ref, ref, send, recv, pair)
 
     def goes(way, step, i):
         return step < 4 or (way == 0) == (i < 2)
@@ -122,15 +126,14 @@
 
     @pl.when(jnp.logical_not(carrier))
     def _():
-        for i in (2, 3):
-            pair_copy(z, i).start()
+        pair_copy(z, 0).start()
 
     @pl.when(carrier)
     def _():
         for i in (0, 1):
             for way in range(2):
                 ring_copy(way, 1, i, z).start()
-            pair_copy(z, i).start()
+        pair_copy(z, 1).start()
 
     @pl.when(swaps)
     def _():
@@ -139,8 +142,8 @@
 
     @pl.when(carrier)
     def _():
+        pair_copy(z, 0).wait_recv()
         for i in (2, 3):
-            pair_copy(z, i).wait_recv()
             for way in range(2):
                 ring_copy(way, 1, i, z).start()
 
@@ -157,7 +160,7 @@
                     part = blocks.at[(1 - half) * NZ + zb, pl.ds(start, size), :]
                     to = on_ring(lax.rem(z + (1 if way == 0 else NZ - 1), NZ))
                     slot = 4 * (step - 1) + 2 * half + i
-                    came = copy(part, part, ring_send.at[way, slot], ring_recv.at[way, slot], to)
+                    came = copy(part, part, ring_send, ring_recv.at[way, slot], to)
                     came.wait_recv()
                     last = step == 3
                     far = 12 + i
@@ -165,10 +168,10 @@
 
                     @pl.when(jnp.logical_or(jnp.logical_not(last), (half == 0) == (way == 0)))
                     def _():
-                        copy(part, part, ring_send.at[way, slot], ring_recv.at[way, slot], to).start()
-
-                    at = 4 * zb + 2 * half + i
-                    copy(part, part, d2d_send.at[at], d2d_recv.at[at], pair).start()
+                        copy(part, part, ring_send, ring_recv.at[way, slot], to).start()
+
+            for way in range(2):
+                pair_copy(origin(way, step), 1 - half).start()
 
     def receive_far():
         @pl.when(carrier)
@@ -177,7 +180,8 @@
                 way = 0 if i < 2 else 1
                 zb = origin(way, 4)
                 ring_copy(way, 4, i, zb).wait_recv()
-                pair_copy(zb, i).start()
+                if i % 2 == 1:
+                    pair_copy(zb, 1 - way).start()
 
     def prepare():
         @pl.when(swaps)
@@ -237,15 +241,13 @@
         off = n // 2
         zb = lax.rem(z + jnp.where(half == 0, NZ - off, off), NZ)
 
-        @pl.when(jnp.logical_not(carrier))
-        def _():
-            for i in range(2):
-                pair_copy(zb, i).wait_recv()
-
-            @pl.when(n > 1)
-            def _():
-                for i in (2, 3):
-                    pair_copy(zb, i).wait_recv()
+        @pl.when(jnp.logical_and(jnp.logical_not(carrier), n == 1))
+        def _():
+            pair_copy(z, 1).wait_recv()
+
+        @pl.when(jnp.logical_and(jnp.logical_not(carrier), n > 1))
+        def _():
+            bytes_of(blocks.at[pl.ds(0, 2)], d2d_send, d2d_recv.at[zb]).wait_recv()
 
         scores(zb)
         return carry
@@ -275,25 +277,21 @@
             key=lambda d: -min(d[0], 4 - d[0]) - min(d[1], 4 - d[1]),
         )
         return [
-            copy(slot, slot, row_send.at[phase, k], row_recv.at[phase, me], off_plane(*d)) for k, d in enumerate(ways)
+            copy(slot, slot, row_send.at[phase], row_recv.at[phase], off_plane(*d)) for d in ways
         ]
+
+    def plane_bytes(phase):
+        return bytes_of(row_buf.at[phase, pl.ds(0, NP - 1)], row_send.at[phase], row_recv.at[phase])
 
     def across_plane(phase, meanwhile):
         for c in plane_copies(phase):
             c.start()
         meanwhile()
 
-        def arrive(k, carry):
-            q = lax.rem(me + k, NP)
-            slot = row_buf.at[phase, q]
-            copy(slot, slot, row_send.at[phase, 0], row_recv.at[phase, q], pair).wait_recv()
-            return carry
-
-        lax.fori_loop(1, NP, arrive, 0)
+        plane_bytes(phase).wait_recv()
 
     def plane_sent(phase):
-        for c in plane_copies(phase):
-            c.wait_send()
+        plane_bytes(phase).wait_send()
 
     QUAD = 4
     TALL = 256
@@ -385,18 +383,13 @@
     def ring_copies(q):
         part = z_buf.at[z, pl.ds(8 * q, 8), :]
         return [
-            copy(part, part, z_send.at[q, k], z_recv.at[q, z], on_ring(lax.rem(z + k, NZ))) for k in (4, 3, 5, 2, 6, 1, 7)
+            copy(part, part, z_send.at[q], z_recv.at[q], on_ring(lax.rem(z + k, NZ))) for k in (4, 3, 5, 2, 6, 1, 7)
         ]
 
-    def ring_waits(slots):
-        def arrive(k, carry):
-            other = lax.rem(z + k, NZ)
-            for phase, ref in slots:
-                part = ref(other)
-                copy(part, part, z_send.at[phase, 0], z_recv.at[phase, other], pair).wait_recv()
-            return carry
-
-        lax.fori_loop(1, NZ, arrive, 0)
+    def ring_bytes(phase):
+        others = pl.ds(0, NZ - 1)
+        ref = fin_buf.at[others] if phase == 2 else z_buf.at[others, pl.ds(0, 8), :]
+        return bytes_of(ref, z_send.at[phase], z_recv.at[phase])
 
     with jax.named_scope("row_lse"):
         for r in range(ROWS // LANES):
@@ -413,19 +406,12 @@
 
         @pl.when(carrier)
         def _():
-            for step in range(1, 5):
-                for i in range(4):
-                    for way in range(2):
-                        if goes(way, step, i):
-                            ring_copy(way, step, i, z).wait_send()
-                            pair_copy(origin(way, step), i).wait_send()
-            for i in range(2):
-                pair_copy(z, i).wait_send()
+            bytes_of(blocks.at[pl.ds(0, 14)], ring_send, d2d_recv.at[0]).wait_send()
+            bytes_of(blocks.at[pl.ds(0, 15)], d2d_send, d2d_recv.at[0]).wait_send()
 
         @pl.when(jnp.logical_not(carrier))
         def _():
-            for i in (2, 3):
-                pair_copy(z, i).wait_send()
+            pair_copy(z, 0).wait_send()
 
     with jax.named_scope("plane_0"):
         across_plane(0, after_gather)
@@ -445,7 +431,8 @@
     with jax.named_scope("exp"):
         with_pair(0, first_columns, to_ring)
     with jax.named_scope("ring_0"):
-        ring_waits([(q, lambda other, q=q: z_buf.at[other, pl.ds(8 * q, 8), :]) for q in range(2)])
+        for q in range(2):
+            ring_bytes(q).wait_recv()
     delta[halves(core), :] = -log_src - lse2([z_buf[k] for k in range(NZ)])
     half = delta.at[halves(core), :]
     give = copy(half, half, pair_send.at[4], pair_recv.at[4], pair)
@@ -472,8 +459,7 @@
     def after_ring():
         plane_sent(0)
         for q in range(2):
-            for c in ring_copies(q):
-                c.wait_send()
+            ring_bytes(q).wait_send()
 
     with jax.named_scope("plane_1"):
         across_plane(1, after_ring)
@@ -485,7 +471,7 @@
     hand.start()
 
     def part_copy(to):
-        return copy(own_buf.at[to], fin_buf.at[z], z_send.at[2, to], z_recv.at[2, z], on_ring(to))
+        return copy(own_buf.at[to], fin_buf.at[z], z_send.at[2], z_recv.at[2], on_ring(to))
 
     def to_owners(q, joined):
         for i in range(NZ // 2):
@@ -507,13 +493,9 @@
         plane_sent(1)
         hand.wait()
         f_ref[...] = jnp.where(swaps, f_pair[...], f_own[...])
-        ring_waits([(2, lambda other: fin_buf.at[other])])
+        ring_bytes(2).wait_recv()
     g_ref[...] = g0[...] - (log_src + lse2([fin_buf[k] for k in range(NZ)])) / SCALE
-    for to in range(NZ):
-
-        @pl.when(z != to)
-        def _():
-            part_copy(to).wait_send()
+    ring_bytes(2).wait_send()
 
 
 def body(sources, targets, duals_init):
@@ -549,8 +531,8 @@
             pltpu.VMEM((NZ, 2, LANES), F32),
             pltpu.VMEM((8, LANES), F32),
             pltpu.VMEM((8, LANES), F32),
-            dma((2, 14)), dma((2, 14)), dma((32,)), dma((32,)), dma((2,)), dma((2,)),
-            dma((2, NP)), dma((2, NP)), dma((3, NZ)), dma((3, NZ)), dma((6,)), dma((6,)),
+            dma, dma((2, 14)), dma, dma((NZ,)), dma((2,)), dma((2,)),
+            dma((2,)), dma((2,)), dma((3,)), dma((3,)), dma((6,)), dma((6,)),
         ],
         compiler_params=pltpu.CompilerParams(
             collective_id=0, has_side_effects=True, vmem_limit_bytes=60 * 1024 * 1024

time: 57.6 us -> 55.9 us (0.970)
  Pallas kernels: 55.7 us -> 54 us
    pallas_call x1, Pallas kernels: 55.7 us -> 54 us  [body(): pl.pallas_call(functools.partial(kernel, math.log2(n_src), math.log2(n_ds...]
where the time goes in v4:
time: 55.9 us; the launch traced here: 55.8 us
  Pallas kernels  54 us (97%)
  local copies, waits for them, and re-layouts  1.16 us (2%)
  between operations  0.64 us (1%)
    pallas_call x1, Pallas kernels, body(): pl.pallas_call(functools.partial(kernel, math.log2(n_src), math.log2(n_ds...  54 us
    unnamed x2, local copies, waits for them, and re-layouts  1.16 us

profile of v4, /device:TPU:1, one launch (start us, length us, event | category | flops | bytes accessed | tf_op | source)
XLA Modules:
  0.0 55.8 jit_solution(13930673396108870387)
XLA Ops:
  0.6 54.0 %sinkhorn.1 = (f32[8,128]{1,0:T(8,128)S(1)}, f32[2,128]{1,0:T(2,128)S(1)}) custom-call(f32[1024,128]{1,0:T(8,128)} %src_ref.1, f32[256,128]{1,0:T(8,128)} %tgt_ref.1, f32[2,128]{1,0:T(2,128)} %bitcast.5), custom_call_target="tpu_custom_call" | custom-call | tf_op jit(solution)/shard_map/sinkhorn/pallas_call | solution.py:506
  54.6 0.6 %copy.7 = f32[1024]{0:T(1024)} copy(f32[1024]{0:T(1024)S(1)} %bitcast.3) | data formatting | bytes 8192
  55.2 0.6 %copy.8 = f32[256]{0:T(256)} copy(f32[256]{0:T(256)S(1)} %bitcast.4) | data formatting | bytes 2048

commit v5 on v4

--- a/solution.py
+++ b/solution.py
@@ -37,7 +37,7 @@
     g0, load_sem, tile, kern, blocks, rows_in, lhs, acc, wide,
     top, row_stat, col_stat, gamma, delta, weight,
     row_buf, pair_buf, z_buf, own_buf, fin_buf, f_own, f_pair,
-    ring_send, ring_recv, d2d_send, d2d_recv, x_send, x_recv,
+    met, ring_send, ring_recv, d2d_send, d2d_recv, x_send, x_recv,
     row_send, row_recv, z_send, z_recv, pair_send, pair_recv,
 ):
     blk, tgt = lax.axis_index("blk"), lax.axis_index("tgt")
@@ -46,8 +46,11 @@
     pair = (blk, tgt + 1 - 2 * core)
     me = x_lo * 8 + tgt // 2
 
-    def on_plane(q):
-        return (q // 8) * NZ + z, lax.rem(q, 8) * 2 + core
+    x_at = 2 * x_hi + x_lo
+
+    def off_plane(dx, dy):
+        x, row = lax.rem(x_at + dx, 4), lax.rem(y + dy, 4)
+        return lax.rem(x, 2) * NZ + z, row * 4 + (x // 2) * 2 + core
 
     def on_ring(other):
         return x_lo * NZ + other, tgt
@@ -69,11 +72,9 @@
     loads[1].start()
 
     barrier = pltpu.get_barrier_semaphore()
-    for k in range(1, NP):
-        pl.semaphore_signal(barrier, inc=1, device_id=on_plane(lax.rem(me + k, NP)), device_id_type=MESH)
-    for k in range(1, NZ):
-        pl.semaphore_signal(barrier, inc=1, device_id=on_ring(lax.rem(z + k, NZ)), device_id_type=MESH)
-    pl.semaphore_signal(barrier, inc=1, device_id=pair, device_id_type=MESH)
+    around = [off_plane(dx, dy) for dx, dy in ((1, 0), (3, 0), (0, 1), (0, 3))]
+    for there in (on_ring(lax.rem(z + 1, NZ)), on_ring(lax.rem(z + NZ - 1, NZ)), pair, *around):
+        pl.semaphore_signal(barrier, inc=1, device_id=there, device_id_type=MESH)
 
     @pl.when(swaps)
     def _():
@@ -92,7 +93,7 @@
         blocks[own, half : half + 1, :] = SCALE * (g0[half : half + 1, :] - norm)
 
     with jax.named_scope("barrier"):
-        pl.semaphore_wait(barrier, NP - 1 + NZ - 1 + 1 + 2 * swaps.astype(jnp.int32))
+        pl.semaphore_wait(barrier, 7 + 2 * swaps.astype(jnp.int32))
 
     def copy(src, dst, send, recv, where):
         return pltpu.make_async_remote_copy(
@@ -146,6 +147,15 @@
         for i in (2, 3):
             for way in range(2):
                 ring_copy(way, 1, i, z).start()
+
+    def greet(r):
+        for there in around:
+            pl.semaphore_signal(met.at[r], inc=1, device_id=there, device_id_type=MESH)
+
+    def hear(r):
+        pl.semaphore_wait(met.at[r], len(around))
+
+    greet(0)
 
     def origin(way, step):
         return lax.rem(z + (NZ - step if way == 0 else step), NZ)
@@ -250,6 +260,12 @@
             bytes_of(blocks.at[pl.ds(0, 2)], d2d_send, d2d_recv.at[zb]).wait_recv()
 
         scores(zb)
+
+        @pl.when(jnp.logical_or(n == 1, n == 3))
+        def _():
+            hear(n // 2)
+            greet(n // 2 + 1)
+
         return carry
 
     with jax.named_scope("receive_1"):
@@ -259,16 +275,11 @@
         prepare()
     with jax.named_scope("scores"):
         lax.fori_loop(1, NZ + 1, scores_step, 0)
+        hear(2)
 
     def spread(row):
         for r in range(ROWS // LANES):
             wide[r * LANES : (r + 1) * LANES, :] = jnp.broadcast_to(row[r : r + 1, :], (LANES, LANES)).T
-
-    x_at = 2 * x_hi + x_lo
-
-    def off_plane(dx, dy):
-        x, row = lax.rem(x_at + dx, 4), lax.rem(y + dy, 4)
-        return lax.rem(x, 2) * NZ + z, row * 4 + (x // 2) * 2 + core
 
     def plane_copies(phase):
         slot = row_buf.at[phase, me]
@@ -531,7 +542,7 @@
             pltpu.VMEM((NZ, 2, LANES), F32),
             pltpu.VMEM((8, LANES), F32),
             pltpu.VMEM((8, LANES), F32),
-            dma, dma((2, 14)), dma, dma((NZ,)), dma((2,)), dma((2,)),
+            pltpu.SemaphoreType.REGULAR((3,)), dma, dma((2, 14)), dma, dma((NZ,)), dma((2,)), dma((2,)),
             dma((2,)), dma((2,)), dma((3,)), dma((3,)), dma((6,)), dma((6,)),
         ],
         compiler_params=pltpu.CompilerParams(

time: 55.9 us -> 54.9 us (0.982)
  Pallas kernels: 54 us -> 53 us
    pallas_call x1, Pallas kernels: 54 us -> 53 us  [body(): pl.pallas_call(functools.partial(kernel, math.log2(n_src), math.log2(n_ds...]
where the time goes in v5:
time: 54.9 us; the launch traced here: 54.8 us
  Pallas kernels  53 us (97%)
  local copies, waits for them, and re-layouts  1.16 us (2%)
  between operations  0.64 us (1%)
    pallas_call x1, Pallas kernels, body(): pl.pallas_call(functools.partial(kernel, math.log2(n_src), math.log2(n_ds...  53 us
    unnamed x2, local copies, waits for them, and re-layouts  1.16 us

profile of v5, /device:TPU:1, one launch (start us, length us, event | category | flops | bytes accessed | tf_op | source)
XLA Modules:
  0.0 54.8 jit_solution(10135797704959051249)
XLA Ops:
  0.6 53.0 %sinkhorn.1 = (f32[8,128]{1,0:T(8,128)S(1)}, f32[2,128]{1,0:T(2,128)S(1)}) custom-call(f32[1024,128]{1,0:T(8,128)} %src_ref.1, f32[256,128]{1,0:T(8,128)} %tgt_ref.1, f32[2,128]{1,0:T(2,128)} %bitcast.5), custom_call_target="tpu_custom_call" | custom-call | tf_op jit(solution)/shard_map/sinkhorn/pallas_call | solution.py:517
  53.6 0.6 %copy.7 = f32[1024]{0:T(1024)} copy(f32[1024]{0:T(1024)S(1)} %bitcast.3) | data formatting | bytes 8192
  54.2 0.6 %copy.8 = f32[256]{0:T(256)} copy(f32[256]{0:T(256)S(1)} %bitcast.4) | data formatting | bytes 2048

commit v6 on v5

--- a/solution.py
+++ b/solution.py
@@ -52,15 +52,16 @@
         x, row = lax.rem(x_at + dx, 4), lax.rem(y + dy, 4)
         return lax.rem(x, 2) * NZ + z, row * 4 + (x // 2) * 2 + core
 
+    def same_rows(dx, dy):
+        blk_there, tgt_there = off_plane(dx, dy)
+        return blk_there, tgt_there if dx % 2 == 0 else tgt_there + 1 - 2 * core
+
     def on_ring(other):
         return x_lo * NZ + other, tgt
 
-    def beside(step):
-        x = lax.rem(2 * x_hi + x_lo + step + 4, 4)
-        return lax.rem(x, 2) * NZ + z, y * 4 + (x // 2) * 2 + x_lo
-
-    swaps = core != x_lo
-    left, right = beside(-1), beside(1)
+    carrier = core == 1
+    swaps = core == 0
+    left, right = off_plane(3, 0), off_plane(1, 0)
     own = core * NZ + z
 
     loads = [
@@ -76,11 +77,6 @@
     for there in (on_ring(lax.rem(z + 1, NZ)), on_ring(lax.rem(z + NZ - 1, NZ)), pair, *around):
         pl.semaphore_signal(barrier, inc=1, device_id=there, device_id_type=MESH)
 
-    @pl.when(swaps)
-    def _():
-        for there in (left, right):
-            pl.semaphore_signal(barrier, inc=1, device_id=there, device_id_type=MESH)
-
     @pl.when(jnp.logical_not(swaps))
     def _():
         loads[2].start()
@@ -93,7 +89,7 @@
         blocks[own, half : half + 1, :] = SCALE * (g0[half : half + 1, :] - norm)
 
     with jax.named_scope("barrier"):
-        pl.semaphore_wait(barrier, 7 + 2 * swaps.astype(jnp.int32))
+        pl.semaphore_wait(barrier, 7)
 
     def copy(src, dst, send, recv, where):
         return pltpu.make_async_remote_copy(
@@ -106,7 +102,7 @@
 
     def ring_copy(way, step, i, zb):
         to = on_ring(lax.rem(z + (1 if way == 0 else NZ - 1), NZ))
-        slot = 4 * (step - 1) + (i if step < 4 else i % 2)
+        slot = 4 * (step - 1) + (i if step < 4 else i // 2)
         return copy(piece(zb, i), piece(zb, i), ring_send, ring_recv.at[way, slot], to)
 
     def pair_copy(zb, of):
@@ -117,13 +113,11 @@
         return copy(ref, ref, send, recv, pair)
 
     def goes(way, step, i):
-        return step < 4 or (way == 0) == (i < 2)
+        return step < 4 or i % 2 == way
 
     def swap_copy(side):
         at = pl.ds(side * (ROWS // 2), ROWS // 2)
         return copy(src_ref.at[at, :], rows_in.at[at, :], x_send.at[side], x_recv.at[side], (left, right)[side])
-
-    carrier = core == 1
 
     @pl.when(jnp.logical_not(carrier))
     def _():
@@ -173,10 +167,9 @@
                     came = copy(part, part, ring_send, ring_recv.at[way, slot], to)
                     came.wait_recv()
                     last = step == 3
-                    far = 12 + i
-                    slot = jnp.where(last, far, slot + 4)
-
-                    @pl.when(jnp.logical_or(jnp.logical_not(last), (half == 0) == (way == 0)))
+                    slot = jnp.where(last, 12 + half, slot + 4)
+
+                    @pl.when(jnp.logical_or(jnp.logical_not(last), i == way))
                     def _():
                         copy(part, part, ring_send, ring_recv.at[way, slot], to).start()
 
@@ -186,12 +179,11 @@
     def receive_far():
         @pl.when(carrier)
         def _():
-            for i in range(4):
-                way = 0 if i < 2 else 1
-                zb = origin(way, 4)
-                ring_copy(way, 4, i, zb).wait_recv()
-                if i % 2 == 1:
-                    pair_copy(zb, 1 - way).start()
+            far = origin(0, 4)
+            for half in range(2):
+                for way in range(2):
+                    ring_copy(way, 4, 2 * half + way, far).wait_recv()
+                pair_copy(far, 1 - half).start()
 
     def prepare():
         @pl.when(swaps)
@@ -237,14 +229,18 @@
             acc[rows, :] = acc[rows, :] * jnp.exp2(old - new) + ((e[0] + e[1]) + (e[2] + e[3]))
 
     def scores_step(n, carry):
-        step = n // 2 + 1
         half = lax.rem(n, 2)
 
-        @pl.when(jnp.logical_and(n >= 2, n < 6))
-        def _():
-            receive(step, half)
-
-        @pl.when(n == 2 * NZ // 2)
+        @pl.when(n == 2)
+        def _():
+            receive(1, 0)
+            receive(1, 1)
+
+        @pl.when(jnp.logical_and(n >= 3, n < 7))
+        def _():
+            receive((n + 1) // 2, 1 - half)
+
+        @pl.when(n == NZ)
         def _():
             receive_far()
 
@@ -268,9 +264,6 @@
 
         return carry
 
-    with jax.named_scope("receive_1"):
-        receive(1, 0)
-        receive(1, 1)
     with jax.named_scope("prepare"):
         prepare()
     with jax.named_scope("scores"):
@@ -288,7 +281,7 @@
             key=lambda d: -min(d[0], 4 - d[0]) - min(d[1], 4 - d[1]),
         )
         return [
-            copy(slot, slot, row_send.at[phase], row_recv.at[phase], off_plane(*d)) for d in ways
+            copy(slot, slot, row_send.at[phase], row_recv.at[phase], same_rows(*d)) for d in ways
         ]
 
     def plane_bytes(phase):

time: 54.9 us -> 53.2 us (0.969)
  Pallas kernels: 53 us -> 51.3 us
    pallas_call x1, Pallas kernels: 53 us -> 51.3 us  [body(): pl.pallas_call(functools.partial(kernel, math.log2(n_src), math.log2(n_ds...]
where the time goes in v6:
time: 53.2 us; the launch traced here: 53.1 us
  Pallas kernels  51.3 us (96%)
  local copies, waits for them, and re-layouts  1.16 us (2%)
  between operations  0.64 us (1%)
    pallas_call x1, Pallas kernels, body(): pl.pallas_call(functools.partial(kernel, math.log2(n_src), math.log2(n_ds...  51.3 us
    unnamed x2, local copies, waits for them, and re-layouts  1.16 us

profile of v6, /device:TPU:1, one launch (start us, length us, event | category | flops | bytes accessed | tf_op | source)
XLA Modules:
  0.0 53.1 jit_solution(6277741816728065342)
XLA Ops:
  0.6 51.3 %sinkhorn.1 = (f32[8,128]{1,0:T(8,128)S(1)}, f32[2,128]{1,0:T(2,128)S(1)}) custom-call(f32[1024,128]{1,0:T(8,128)} %src_ref.1, f32[256,128]{1,0:T(8,128)} %tgt_ref.1, f32[2,128]{1,0:T(2,128)} %bitcast.5), custom_call_target="tpu_custom_call" | custom-call | tf_op jit(solution)/shard_map/sinkhorn/pallas_call | solution.py:510
  51.9 0.6 %copy.7 = f32[1024]{0:T(1024)} copy(f32[1024]{0:T(1024)S(1)} %bitcast.3) | data formatting | bytes 8192
  52.5 0.6 %copy.8 = f32[256]{0:T(256)} copy(f32[256]{0:T(256)S(1)} %bitcast.4) | data formatting | bytes 2048

commit v7 on v6

--- a/solution.py
+++ b/solution.py
@@ -34,7 +34,7 @@
 def kernel(
     log_src, log_dst,
     src_ref, tgt_ref, g0_ref, f_ref, g_ref,
-    g0, load_sem, tile, kern, blocks, rows_in, lhs, acc, wide,
+    g0, load_sem, stage, tile, kern, blocks, rows_in, lhs, acc, wide,
     top, row_stat, col_stat, gamma, delta, weight,
     row_buf, pair_buf, z_buf, own_buf, fin_buf, f_own, f_pair,
     met, ring_send, ring_recv, d2d_send, d2d_recv, x_send, x_recv,
@@ -68,9 +68,14 @@
         pltpu.make_async_copy(tgt_ref, blocks.at[own, pl.ds(HEAD, COLS), :], load_sem.at[0]),
         pltpu.make_async_copy(g0_ref, g0, load_sem.at[1]),
         pltpu.make_async_copy(src_ref, rows_in, load_sem.at[2]),
+        pltpu.make_async_copy(src_ref, stage, load_sem.at[2]),
     ]
     loads[0].start()
     loads[1].start()
+
+    @pl.when(swaps)
+    def _():
+        loads[3].start()
 
     barrier = pltpu.get_barrier_semaphore()
     around = [off_plane(dx, dy) for dx, dy in ((1, 0), (3, 0), (0, 1), (0, 3))]
@@ -117,7 +122,7 @@
 
     def swap_copy(side):
         at = pl.ds(side * (ROWS // 2), ROWS // 2)
-        return copy(src_ref.at[at, :], rows_in.at[at, :], x_send.at[side], x_recv.at[side], (left, right)[side])
+        return copy(stage.at[at, :], rows_in.at[at, :], x_send.at[side], x_recv.at[side], (left, right)[side])
 
     @pl.when(jnp.logical_not(carrier))
     def _():
@@ -132,6 +137,7 @@
 
     @pl.when(swaps)
     def _():
+        loads[3].wait()
         for side in range(2):
             swap_copy(side).start()
 
@@ -515,6 +521,7 @@
         scratch_shapes=[
             pltpu.VMEM((2, LANES), F32),
             dma((3,)),
+            pltpu.VMEM((ROWS, D), F32),
             pltpu.VMEM((BLOCKS, ROWS, COLS), F32),
             pltpu.VMEM((BLOCKS, ROWS, COLS), F32),
             pltpu.VMEM((BLOCKS, HEAD + COLS, D), F32),

time: 53.2 us -> 53.2 us (level)
  no operation moved by 1% of the time
where the time goes in v7:
time: 53.2 us; the launch traced here: 53.1 us
  Pallas kernels  51.3 us (96%)
  local copies, waits for them, and re-layouts  1.16 us (2%)
  between operations  0.64 us (1%)
    pallas_call x1, Pallas kernels, body(): pl.pallas_call(functools.partial(kernel, math.log2(n_src), math.log2(n_ds...  51.3 us
    unnamed x2, local copies, waits for them, and re-layouts  1.16 us

profile of v7, /device:TPU:1, one launch (start us, length us, event | category | flops | bytes accessed | tf_op | source)
XLA Modules:
  0.0 53.1 jit_solution(9791036373076689741)
XLA Ops:
  0.6 51.3 %sinkhorn.1 = (f32[8,128]{1,0:T(8,128)S(1)}, f32[2,128]{1,0:T(2,128)S(1)}) custom-call(f32[1024,128]{1,0:T(8,128)} %src_ref.1, f32[256,128]{1,0:T(8,128)} %tgt_ref.1, f32[2,128]{1,0:T(2,128)} %bitcast.5), custom_call_target="tpu_custom_call" | custom-call | tf_op jit(solution)/shard_map/sinkhorn/pallas_call | solution.py:516
  51.9 0.6 %copy.7 = f32[1024]{0:T(1024)} copy(f32[1024]{0:T(1024)S(1)} %bitcast.3) | data formatting | bytes 8192
  52.5 0.6 %copy.8 = f32[256]{0:T(256)} copy(f32[256]{0:T(256)S(1)} %bitcast.4) | data formatting | bytes 2048
